TPU v7x, 256 devices: a whole 4x4x8 slice. The times are simulated.
256 devices in a mesh: member: 8 (over y, x_lo), space: 32 (over z, x_hi, core).
Axes of the slice: x: 4 (x_hi: 2, x_lo: 2; x = x_hi * 2 + x_lo), y: 4, z: 8, core: 2. Of those that a mesh axis runs over, the one named last changes fastest.
Arguments:
- hidden_codes: bfloat16 [16, 256, 92160], P('member', None, 'space'), may hold values from -6 to 6
- w_in: bfloat16 [1024, 256], replicated, may hold values from -0.375 to 0.375
- b_in: float32 [1024], replicated, may hold values from -3 to 3
- w_out: bfloat16 [72, 1024], replicated, may hold values from -0.1875 to 0.1875
- b_out: float32 [72], replicated, may hold values from -3 to 3
- target: bfloat16 [72, 92160], P(None, 'space'), may hold values from -6 to 6
- band_start: int32 [32], P('space'), may hold values from 0 to 62, as said below
Outputs:
- code_sensitivity: bfloat16 [16, 256, 92160], P('member', None, 'space')
- grad_w_in: float32 [1024, 256], replicated
- grad_w_out: float32 [72, 1024], replicated
- grad_b_in: float32 [1024], replicated
Inputs may be any that keep to these rules, and one draw needn't show every extreme that they name: band_start holds each of 0, 2, 4, ... once, in some order.
All inputs are finite; a program needn't handle non-finite values.
Results may differ from a plain program's by a relative error of at most 0.005.
The roundings to bfloat16 on the way count: a program that leaves them out, or rounds other values in their place, can miss the bound.
Values may be sent and summed in bfloat16 or wider, within the bound.
A program may use at most 128 MiB of HBM per device.

v0:
```python
import math

import jax
import jax.numpy as jnp
from jax import lax
from jax.sharding import PartitionSpec as P

LON = 1440


def split_up(array, dim, devices):
    dims = array.shape
    parts = array.reshape(*dims[:dim], devices, dims[dim] // devices, *dims[dim + 1 :])
    return jnp.moveaxis(parts, dim, 0)


def edges_of(length, count):
    unit = 8 if length >= 8 * count else 1
    return [length // unit * k // count * unit for k in range(1, count)]


def joined_along(parts, dim):
    dims = list(parts.shape[1:])
    dims[dim] *= parts.shape[0]
    return jnp.moveaxis(parts, 0, dim).reshape(dims)


def exchange_in_pieces(array, axis, pieces, split_dim, concat_dim):
    parts = split_up(array, split_dim, lax.axis_size(axis))
    cut = max(range(1, max(2, parts.ndim - 1)), key=lambda d: parts.shape[d])
    gathered = []
    for piece in jnp.split(parts, edges_of(parts.shape[cut], pieces), axis=cut):
        if piece.size:
            gathered.append(lax.all_to_all(piece, axis, split_axis=0, concat_axis=0, tiled=True))
    return joined_along(jnp.concatenate(gathered, axis=cut), concat_dim)


def sent_and_summed(array, axis, dim):
    devices = lax.axis_size(axis)
    parts = lax.all_to_all(split_up(array, dim, devices), axis, 0, 0, tiled=True)
    return jnp.sum(parts.astype(jnp.float32), axis=0)


def copy_for_each(array, axis):
    devices = lax.axis_size(axis)
    return lax.all_to_all(
        jnp.broadcast_to(array[None], (devices, *array.shape)), axis, 0, 0, tiled=True
    )


def of_everyone(array, axis):
    everything = copy_for_each(array, axis)
    return jnp.sum(everything, axis=0)


def gathered_copies(array, axis, dim):
    parts = copy_for_each(array, axis)
    return joined_along(parts, dim)


def slope(diff):
    return diff / jnp.sqrt(diff * diff + 0.0625)


def pairwise_total(values, tiles):

    def lone_realization(total, other):
        return (total + slope(values - other.astype(jnp.float32)[None]), None)

    total, discarded_value = lax.scan(lone_realization, jnp.zeros_like(values), tiles)
    return total


def on_device(hidden_codes, w_in, b_in, w_out, b_out, target, band_start):
    local_members = hidden_codes.shape[0]
    cells = hidden_codes.shape[2]
    rows = cells // LON
    lat_rows = rows * lax.axis_size("space")
    members = local_members * lax.axis_size("member")
    angle = ((band_start[0] + jnp.arange(rows, dtype=jnp.int32)).astype(jnp.float32) + 0.5) * (
        math.pi / lat_rows
    ) - math.pi / 2
    area = jnp.broadcast_to(jnp.cos(angle)[:, None], (rows, LON)).reshape(cells)
    saved = []
    mapped_predictions = []
    for ensemble_position in range(local_members):
        pre = (
            jnp.dot(w_in, hidden_codes[ensemble_position], preferred_element_type=jnp.float32)
            + b_in[:, None]
        )
        act_f, undo = jax.vjp(jax.nn.gelu, pre)
        act = act_f.astype(jnp.bfloat16)
        saved.append((act, undo))
        mapped_predictions.append(
            (jnp.dot(w_out, act, preferred_element_type=jnp.float32) + b_out[:, None]).astype(
                jnp.bfloat16
            )
        )
    predicted_maps = jnp.stack(mapped_predictions)
    diagonal_contribution = predicted_maps.astype(jnp.float32)
    block = lax.all_to_all(predicted_maps, "member", split_axis=2, concat_axis=0, tiled=True)
    total = pairwise_total(block.astype(jnp.float32), block)
    couple_index = exchange_in_pieces(total, "member", 2, 0, 2)
    goal = target.astype(jnp.float32)[None]
    prediction_sensitivity = (
        area[None, None, :] * (slope(diagonal_contribution - goal) - couple_index / members)
    ).astype(jnp.bfloat16)
    adjoint_entry_matrix = jnp.zeros(w_in.shape, jnp.float32)
    adjoint_exit_matrix = jnp.zeros(w_out.shape, jnp.float32)
    g_bias = jnp.zeros(b_in.shape, jnp.float32)
    grads = []
    for ensemble_position in range(local_members):
        act, undo = saved[ensemble_position]
        prediction_adjoint = prediction_sensitivity[ensemble_position]
        dact = jnp.dot(w_out.T, prediction_adjoint, preferred_element_type=jnp.float32)
        dpre = undo(dact)[0].astype(jnp.bfloat16)
        grads.append(jnp.dot(w_in.T, dpre, preferred_element_type=jnp.float32).astype(jnp.bfloat16))
        adjoint_entry_matrix = adjoint_entry_matrix + jnp.dot(
            dpre, hidden_codes[ensemble_position].T, preferred_element_type=jnp.float32
        )
        adjoint_exit_matrix = adjoint_exit_matrix + jnp.dot(
            prediction_adjoint, act.T, preferred_element_type=jnp.float32
        )
        g_bias = g_bias + jnp.sum(dpre.astype(jnp.float32), axis=1)
    code_sensitivity = jnp.stack(grads)
    stacked = jnp.concatenate(
        [adjoint_entry_matrix, adjoint_exit_matrix.T, g_bias[:, None]], axis=1
    )
    shares = sent_and_summed(stacked.astype(jnp.bfloat16), "space", 0)
    shares = of_everyone(shares, "member")
    summed = gathered_copies(shares, "space", 0)
    scale = 1.0 / math.sqrt(members * cells)
    latent_width = w_in.shape[1]
    channel_count = w_out.shape[0]
    grad_w_in = summed[:, :latent_width] * scale
    grad_w_out = summed[:, latent_width : latent_width + channel_count].T * scale
    grad_b_in = summed[:, latent_width + channel_count] * scale
    return (code_sensitivity, grad_w_in, grad_w_out, grad_b_in)


def solution(mesh):
    in_specs = (P("member", None, "space"), P(), P(), P(), P(), P(None, "space"), P("space"))
    out_specs = (P("member", None, "space"), P(), P(), P())
    return jax.shard_map(
        on_device, mesh=mesh, in_specs=in_specs, out_specs=out_specs, check_vma=False
    )
```

profile of v0, /device:TPU:1, one launch (start us, length us, event | category | flops | bytes accessed | tf_op | source)
XLA Modules:
  0.0 273.2 jit_solution(17318421373382060209)
XLA Ops:
  1.7 7.5 %fusion.29 = f32[1024,2880]{0,1:T(8,128)} fusion(bf16[1024,256]{1,0:T(8,128)(2,1)S(1)} %copy-done, bf16[2,256,2880]{1,2,0:T(8,128)(2,1)} %param.9), kind=kOutput, calls=%fused_computation.51 | convolution fusion | flops 1509949440 | bytes 13795328 | tf_op jit(solution)/shard_map/dot_general | solution.py:88
  9.2 12.6 %multiply_convert_fusion.1 = (bf16[1024,2880]{0,1:T(8,128)(2,1)S(1)}, bf16[1024,2880]{0,1:T(8,128)(2,1)S(1)}, f32[1024,2880]{0,1:T(8,128)}) fusion(f32[1024]{0:T(1024)S(1)} %copy-done.11, f32[1024,2880]{0,1:T(8,128)} %fusion.29, bf16[1024,256]{1,0:T(8,128)(2,1)S(1)} %copy-done, bf16[2,256,2880]{1,2,0:T(8,128)(2,1)S(1)} %copy-done.7), kind=kOutput, calls=%fused_computation.33 | convolution fusion | flops 1568931840 | bytes 37392384 | tf_op jit(solution)/shard_map/dot_general | solution.py:88
  21.8 1.9 fusion.24
  23.7 1.9 fusion.25
  27.1 2.9 %copy.34 = bf16[2,72,2880]{1,0,2:T(2,128)(2,1)} copy(bf16[2,72,2880]{2,1,0:T(8,128)(2,1)S(1)} %pad_maximum_fusion.1) | data formatting | bytes 1658880 | tf_op jit(solution)/shard_map/stack | solution.py:99
  30.0 5.9 %all-to-all-start = ((bf16[2,72,2880]{1,0,2:T(2,128)(2,1)}), bf16[2,72,2880]{1,0,2:T(2,128)(2,1)S(1)}, u32[]{:S(2)}, u32[]{:S(2)}) async-start(bf16[2,72,2880]{1,0,2:T(2,128)(2,1)} %copy.34), calls=%async_computation | async-start | bytes 2949120 | tf_op jit(solution)/shard_map/all_to_all | solution.py:101
  35.9 19.4 %all-to-all-done = bf16[2,72,2880]{1,0,2:T(2,128)(2,1)S(1)} async-done(((bf16[2,72,2880]{1,0,2:T(2,128)(2,1)}), bf16[2,72,2880]{1,0,2:T(2,128)(2,1)S(1)}, u32[]{:S(2)}, u32[]{:S(2)}) %all-to-all-start) | async-done | bytes 829472 | tf_op jit(solution)/shard_map/all_to_all | solution.py:101
  55.4 1.3 copy.35
  56.9 48.4 %while.11 = (s32[]{:T(128)}, f32[16,72,360]{2,1,0:T(8,128)}, bf16[16,72,360]{2,1,0:T(8,128)(2,1)S(1)}, f32[16,72,360]{2,1,0:T(8,128)S(1)}, s32[]{:T(128)}, /*index=5*/s32[]{:T(128)}) while((s32[]{:T(128)}, f32[16,72,360]{2,1,0:T(8,128)}, bf16[16,72,360]{2,1,0:T(8,128)(2,1)S(1)}, f32[16,72,360]{2,1,0:T(8,128)S(1)}, s32[]{:T(128)}, ...), condition=%wide.region_1.2_spmd.clone, body=%wide.region_0.1_spmd.clone.sunk | while | flops 2514243 | bytes 5235923 | solution.py:70
  56.9 1.6 select_add_fusion.2
  58.6 3.1 %select_add_fusion.2 = f32[16,72,360]{2,1,0:T(8,128)} fusion(f32[16,72,360]{2,1,0:T(8,128)} %get-tuple-element.109, f32[16,72,360]{2,1,0:T(8,128)S(1)} %get-tuple-element.117, f32[72,360]{1,0:T(8,128)S(1)} %bitcast_convert_fusion.3, pred[]{:T(512)S(6)} %compare.3), kind=kLoop, calls=%fused_computation.clone.1 | loop fusion | flops 2488320 | bytes 5080321 | tf_op jit(solution)/shard_map/while/body/eval_jaxpr/add | solution.py:68
  61.7 3.1 %select_add_fusion.2 = f32[16,72,360]{2,1,0:T(8,128)} fusion(f32[16,72,360]{2,1,0:T(8,128)} %get-tuple-element.109, f32[16,72,360]{2,1,0:T(8,128)S(1)} %get-tuple-element.117, f32[72,360]{1,0:T(8,128)S(1)} %bitcast_convert_fusion.3, pred[]{:T(512)S(6)} %compare.3), kind=kLoop, calls=%fused_computation.clone.1 | loop fusion | flops 2488320 | bytes 5080321 | tf_op jit(solution)/shard_map/while/body/eval_jaxpr/add | solution.py:68
  64.8 3.1 %select_add_fusion.2 = f32[16,72,360]{2,1,0:T(8,128)} fusion(f32[16,72,360]{2,1,0:T(8,128)} %get-tuple-element.109, f32[16,72,360]{2,1,0:T(8,128)S(1)} %get-tuple-element.117, f32[72,360]{1,0:T(8,128)S(1)} %bitcast_convert_fusion.3, pred[]{:T(512)S(6)} %compare.3), kind=kLoop, calls=%fused_computation.clone.1 | loop fusion | flops 2488320 | bytes 5080321 | tf_op jit(solution)/shard_map/while/body/eval_jaxpr/add | solution.py:68
  67.9 3.1 %select_add_fusion.2 = f32[16,72,360]{2,1,0:T(8,128)} fusion(f32[16,72,360]{2,1,0:T(8,128)} %get-tuple-element.109, f32[16,72,360]{2,1,0:T(8,128)S(1)} %get-tuple-element.117, f32[72,360]{1,0:T(8,128)S(1)} %bitcast_convert_fusion.3, pred[]{:T(512)S(6)} %compare.3), kind=kLoop, calls=%fused_computation.clone.1 | loop fusion | flops 2488320 | bytes 5080321 | tf_op jit(solution)/shard_map/while/body/eval_jaxpr/add | solution.py:68
  71.0 3.1 %select_add_fusion.2 = f32[16,72,360]{2,1,0:T(8,128)} fusion(f32[16,72,360]{2,1,0:T(8,128)} %get-tuple-element.109, f32[16,72,360]{2,1,0:T(8,128)S(1)} %get-tuple-element.117, f32[72,360]{1,0:T(8,128)S(1)} %bitcast_convert_fusion.3, pred[]{:T(512)S(6)} %compare.3), kind=kLoop, calls=%fused_computation.clone.1 | loop fusion | flops 2488320 | bytes 5080321 | tf_op jit(solution)/shard_map/while/body/eval_jaxpr/add | solution.py:68
  74.1 3.1 %select_add_fusion.2 = f32[16,72,360]{2,1,0:T(8,128)} fusion(f32[16,72,360]{2,1,0:T(8,128)} %get-tuple-element.109, f32[16,72,360]{2,1,0:T(8,128)S(1)} %get-tuple-element.117, f32[72,360]{1,0:T(8,128)S(1)} %bitcast_convert_fusion.3, pred[]{:T(512)S(6)} %compare.3), kind=kLoop, calls=%fused_computation.clone.1 | loop fusion | flops 2488320 | bytes 5080321 | tf_op jit(solution)/shard_map/while/body/eval_jaxpr/add | solution.py:68
  77.3 3.1 %select_add_fusion.2 = f32[16,72,360]{2,1,0:T(8,128)} fusion(f32[16,72,360]{2,1,0:T(8,128)} %get-tuple-element.109, f32[16,72,360]{2,1,0:T(8,128)S(1)} %get-tuple-element.117, f32[72,360]{1,0:T(8,128)S(1)} %bitcast_convert_fusion.3, pred[]{:T(512)S(6)} %compare.3), kind=kLoop, calls=%fused_computation.clone.1 | loop fusion | flops 2488320 | bytes 5080321 | tf_op jit(solution)/shard_map/while/body/eval_jaxpr/add | solution.py:68
  80.4 3.1 %select_add_fusion.2 = f32[16,72,360]{2,1,0:T(8,128)} fusion(f32[16,72,360]{2,1,0:T(8,128)} %get-tuple-element.109, f32[16,72,360]{2,1,0:T(8,128)S(1)} %get-tuple-element.117, f32[72,360]{1,0:T(8,128)S(1)} %bitcast_convert_fusion.3, pred[]{:T(512)S(6)} %compare.3), kind=kLoop, calls=%fused_computation.clone.1 | loop fusion | flops 2488320 | bytes 5080321 | tf_op jit(solution)/shard_map/while/body/eval_jaxpr/add | solution.py:68
  83.5 3.1 %select_add_fusion.2 = f32[16,72,360]{2,1,0:T(8,128)} fusion(f32[16,72,360]{2,1,0:T(8,128)} %get-tuple-element.109, f32[16,72,360]{2,1,0:T(8,128)S(1)} %get-tuple-element.117, f32[72,360]{1,0:T(8,128)S(1)} %bitcast_convert_fusion.3, pred[]{:T(512)S(6)} %compare.3), kind=kLoop, calls=%fused_computation.clone.1 | loop fusion | flops 2488320 | bytes 5080321 | tf_op jit(solution)/shard_map/while/body/eval_jaxpr/add | solution.py:68
  86.6 3.1 %select_add_fusion.2 = f32[16,72,360]{2,1,0:T(8,128)} fusion(f32[16,72,360]{2,1,0:T(8,128)} %get-tuple-element.109, f32[16,72,360]{2,1,0:T(8,128)S(1)} %get-tuple-element.117, f32[72,360]{1,0:T(8,128)S(1)} %bitcast_convert_fusion.3, pred[]{:T(512)S(6)} %compare.3), kind=kLoop, calls=%fused_computation.clone.1 | loop fusion | flops 2488320 | bytes 5080321 | tf_op jit(solution)/shard_map/while/body/eval_jaxpr/add | solution.py:68
  89.7 3.1 %select_add_fusion.2 = f32[16,72,360]{2,1,0:T(8,128)} fusion(f32[16,72,360]{2,1,0:T(8,128)} %get-tuple-element.109, f32[16,72,360]{2,1,0:T(8,128)S(1)} %get-tuple-element.117, f32[72,360]{1,0:T(8,128)S(1)} %bitcast_convert_fusion.3, pred[]{:T(512)S(6)} %compare.3), kind=kLoop, calls=%fused_computation.clone.1 | loop fusion | flops 2488320 | bytes 5080321 | tf_op jit(solution)/shard_map/while/body/eval_jaxpr/add | solution.py:68
  92.8 3.1 %select_add_fusion.2 = f32[16,72,360]{2,1,0:T(8,128)} fusion(f32[16,72,360]{2,1,0:T(8,128)} %get-tuple-element.109, f32[16,72,360]{2,1,0:T(8,128)S(1)} %get-tuple-element.117, f32[72,360]{1,0:T(8,128)S(1)} %bitcast_convert_fusion.3, pred[]{:T(512)S(6)} %compare.3), kind=kLoop, calls=%fused_computation.clone.1 | loop fusion | flops 2488320 | bytes 5080321 | tf_op jit(solution)/shard_map/while/body/eval_jaxpr/add | solution.py:68
  96.0 3.1 %select_add_fusion.2 = f32[16,72,360]{2,1,0:T(8,128)} fusion(f32[16,72,360]{2,1,0:T(8,128)} %get-tuple-element.109, f32[16,72,360]{2,1,0:T(8,128)S(1)} %get-tuple-element.117, f32[72,360]{1,0:T(8,128)S(1)} %bitcast_convert_fusion.3, pred[]{:T(512)S(6)} %compare.3), kind=kLoop, calls=%fused_computation.clone.1 | loop fusion | flops 2488320 | bytes 5080321 | tf_op jit(solution)/shard_map/while/body/eval_jaxpr/add | solution.py:68
  99.1 3.1 %select_add_fusion.2 = f32[16,72,360]{2,1,0:T(8,128)} fusion(f32[16,72,360]{2,1,0:T(8,128)} %get-tuple-element.109, f32[16,72,360]{2,1,0:T(8,128)S(1)} %get-tuple-element.117, f32[72,360]{1,0:T(8,128)S(1)} %bitcast_convert_fusion.3, pred[]{:T(512)S(6)} %compare.3), kind=kLoop, calls=%fused_computation.clone.1 | loop fusion | flops 2488320 | bytes 5080321 | tf_op jit(solution)/shard_map/while/body/eval_jaxpr/add | solution.py:68
  102.2 3.1 %select_add_fusion.2 = f32[16,72,360]{2,1,0:T(8,128)} fusion(f32[16,72,360]{2,1,0:T(8,128)} %get-tuple-element.109, f32[16,72,360]{2,1,0:T(8,128)S(1)} %get-tuple-element.117, f32[72,360]{1,0:T(8,128)S(1)} %bitcast_convert_fusion.3, pred[]{:T(512)S(6)} %compare.3), kind=kLoop, calls=%fused_computation.clone.1 | loop fusion | flops 2488320 | bytes 5080321 | tf_op jit(solution)/shard_map/while/body/eval_jaxpr/add | solution.py:68
  105.3 2.1 split.8
  107.4 3.7 %all-to-all-start.1 = ((f32[8,2,32,360]{3,2,1,0:T(8,128)}), f32[8,2,32,360]{3,2,1,0:T(8,128)S(1)}, u32[]{:S(2)}, u32[]{:S(2)}) async-start(f32[8,2,32,360]{3,2,1,0:T(8,128)} %split.8), calls=%async_computation.1 | async-start | bytes 1572864 | tf_op jit(solution)/shard_map/all_to_all | solution.py:34
  111.1 2.2 split.9
  113.3 9.3 %all-to-all-done.1 = f32[8,2,32,360]{3,2,1,0:T(8,128)S(1)} async-done(((f32[8,2,32,360]{3,2,1,0:T(8,128)}), f32[8,2,32,360]{3,2,1,0:T(8,128)S(1)}, u32[]{:S(2)}, u32[]{:S(2)}) %all-to-all-start.1) | async-done | bytes 737312 | tf_op jit(solution)/shard_map/all_to_all | solution.py:34
  122.6 3.7 %all-to-all-start.2 = ((f32[8,2,40,360]{3,2,1,0:T(8,128)}), f32[8,2,40,360]{3,2,1,0:T(8,128)S(1)}, u32[]{:S(2)}, u32[]{:S(2)}) async-start(f32[8,2,40,360]{3,2,1,0:T(8,128)} %split.9), calls=%async_computation.2 | async-start | bytes 1966080 | tf_op jit(solution)/shard_map/all_to_all | solution.py:34
  126.3 2.0 convert_element_type.76
  129.2 9.6 %all-to-all-done.2 = f32[8,2,40,360]{3,2,1,0:T(8,128)S(1)} async-done(((f32[8,2,40,360]{3,2,1,0:T(8,128)}), f32[8,2,40,360]{3,2,1,0:T(8,128)S(1)}, u32[]{:S(2)}, u32[]{:S(2)}) %all-to-all-start.2) | async-done | bytes 921632 | tf_op jit(solution)/shard_map/all_to_all | solution.py:34
  139.6 1.7 div.17
  141.3 2.3 multiply_convert_fusion.2
  143.6 11.9 %convert_reduce_fusion = (f32[1024]{0:T(1024)S(1)}, bf16[1024,2880]{0,1:T(8,128)(2,1)S(1)}) fusion(f32[1024,2880]{0,1:T(8,128)} %fusion.29, f32[1024]{0:T(1024)S(1)} %copy-done.11, bf16[72,1024]{1,0:T(8,128)(2,1)S(1)} %copy-done.9, bf16[2,72,2880]{2,1,0:T(8,128)(2,1)S(1)} %multiply_convert_fusion.2), kind=kOutput, calls=%fused_computation.30 | convolution fusion | flops 492502016 | bytes 18274304 | tf_op jit(solution)/shard_map/dot_general | solution.py:115
  155.6 1.2 fusion.48
  156.8 10.4 %convert_reduce_fusion.1 = (f32[1024]{0:T(1024)S(1)}, bf16[1024,2880]{0,1:T(8,128)(2,1)}) fusion(f32[1024,2880]{0,1:T(8,128)S(1)} %bitcast.122, f32[1024]{0:T(1024)S(1)} %copy-done.11, bf16[72,1024]{1,0:T(8,128)(2,1)S(1)} %copy-done.9, bf16[2,72,2880]{2,1,0:T(8,128)(2,1)S(1)} %multiply_convert_fusion.2), kind=kOutput, calls=%fused_computation.31 | convolution fusion | flops 492502016 | bytes 18274304 | tf_op jit(solution)/shard_map/dot_general | solution.py:115
  167.2 1.8 fusion.27
  169.1 1.2 fusion.45
  170.9 4.9 %fusion.38 = bf16[1024,256]{1,0:T(8,128)(2,1)S(1)} fusion(f32[1024,256]{1,0:T(8,128)S(1)} %fusion.27, bf16[1024,2880]{0,1:T(8,128)(2,1)} %get-tuple-element.74, bf16[2,256,2880]{1,2,0:T(8,128)(2,1)} %param.9), kind=kOutput, calls=%fused_computation.58 | convolution fusion | flops 1510473728 | bytes 8945664 | tf_op jit(solution)/shard_map/dot_general | solution.py:118
  176.0 36.3 %all_to_all.43 = bf16[32,32,329]{2,1,0:T(8,128)(2,1)S(1)} all-to-all(bf16[32,32,329]{2,1,0:T(8,128)(2,1)S(1)} %pad_maximum_fusion.2), channel_id=1, replica_groups=mesh['member'=8,'space'=32] {'space'}, dimensions={0} | all-to-all | bytes 1347584 | tf_op jit(solution)/shard_map/all_to_all | solution.py:40
  212.6 10.0 %all_to_all.44 = f32[8,32,329]{2,1,0:T(8,128)S(1)} all-to-all(f32[8,32,329]{2,1,0:T(8,128)S(1)} %broadcast_in_dim.11), channel_id=1, replica_groups=mesh['member'=8,'space'=32] {'member'}, dimensions={0} | all-to-all | bytes 673792 | tf_op jit(solution)/shard_map/all_to_all | solution.py:46
  222.6 1.3 broadcast_in_dim.12
  223.9 7.1 %all-to-all-start.5 = ((f32[32,32,329]{2,1,0:T(8,128)}), f32[32,32,329]{2,1,0:T(8,128)S(1)}, u32[]{:S(2)}, u32[]{:S(2)}) async-start(f32[32,32,329]{2,1,0:T(8,128)} %broadcast_in_dim.12), calls=%async_computation.5 | async-start | bytes 3145728 | tf_op jit(solution)/shard_map/all_to_all | solution.py:46
  231.1 4.4 %fusion.20 = bf16[1,256,2880]{1,2,0:T(8,128)(2,1)S(1)} fusion(bf16[1024,2880]{0,1:T(8,128)(2,1)} %get-tuple-element.74, bf16[1024,256]{1,0:T(8,128)(2,1)S(1)} %copy-done), kind=kOutput, calls=%fused_computation.36 | convolution fusion | flops 1510686720 | bytes 7897088 | tf_op jit(solution)/shard_map/dot_general | solution.py:117
  235.5 4.4 %fusion.21 = bf16[1,256,2880]{1,2,0:T(8,128)(2,1)S(1)} fusion(bf16[1024,2880]{0,1:T(8,128)(2,1)} %copy-done.12, bf16[1024,256]{1,0:T(8,128)(2,1)S(1)} %copy-done), kind=kOutput, calls=%fused_computation.37 | convolution fusion | flops 1510686720 | bytes 7897088 | tf_op jit(solution)/shard_map/dot_general | solution.py:117
  239.8 1.9 pad_maximum_fusion
  241.7 28.6 %all-to-all-done.5 = f32[32,32,329]{2,1,0:T(8,128)S(1)} async-done(((f32[32,32,329]{2,1,0:T(8,128)}), f32[32,32,329]{2,1,0:T(8,128)S(1)}, u32[]{:S(2)}, u32[]{:S(2)}) %all-to-all-start.5) | async-done | bytes 1347616 | tf_op jit(solution)/shard_map/all_to_all | solution.py:46
  (78 shorter events, 7.7 us)
Async XLA Ops:
  0.6 1.0 copy-start
  0.6 8.5 %copy-start.7 = (bf16[2,256,2880]{1,2,0:T(8,128)(2,1)S(1)}, bf16[2,256,2880]{1,2,0:T(8,128)(2,1)}, u32[]{:S(2)}) copy-start(bf16[2,256,2880]{1,2,0:T(8,128)(2,1)} %param.9) | copy-start | bytes 8847364
  0.7 8.5 %copy-start.11 = (f32[1024]{0:T(1024)S(1)}, f32[1024]{0:T(1024)}, u32[]{:S(2)}) copy-start(f32[1024]{0:T(1024)} %param.11) | copy-start | bytes 12292
  9.1 12.6 %copy-start.9 = (bf16[72,1024]{1,0:T(8,128)(2,1)S(1)}, bf16[72,1024]{1,0:T(8,128)(2,1)}, u32[]{:S(2)}) copy-start(bf16[72,1024]{1,0:T(8,128)(2,1)} %param.12) | copy-start | bytes 442372
  9.1 12.6 %copy-start.10 = (f32[72]{0:T(128)S(1)}, f32[72]{0:T(128)}, u32[]{:S(2)}) copy-start(f32[72]{0:T(128)} %param.13) | copy-start | bytes 868
  21.8 3.9 %copy-start.1 = (bf16[1024,2880]{0,1:T(8,128)(2,1)}, bf16[1024,2880]{0,1:T(8,128)(2,1)S(1)}, u32[]{:S(2)}) copy-start(bf16[1024,2880]{0,1:T(8,128)(2,1)S(1)} %get-tuple-element.71) | copy-start | bytes 17694724
  21.8 4.2 %copy-start.2 = (bf16[1024,2880]{0,1:T(8,128)(2,1)}, bf16[1024,2880]{0,1:T(8,128)(2,1)S(1)}, u32[]{:S(2)}) copy-start(bf16[1024,2880]{0,1:T(8,128)(2,1)S(1)} %get-tuple-element.70) | copy-start | bytes 17694724
  23.7 2.5 copy-start.3
  26.2 0.8 copy-start.5
  30.0 25.4 %all-to-all-start = ((bf16[2,72,2880]{1,0,2:T(2,128)(2,1)}), bf16[2,72,2880]{1,0,2:T(2,128)(2,1)S(1)}, u32[]{:S(2)}, u32[]{:S(2)}) async-start(bf16[2,72,2880]{1,0,2:T(2,128)(2,1)} %copy.34), calls=%async_computation | async-start | bytes 2949120 | tf_op jit(solution)/shard_map/all_to_all | solution.py:101
  107.4 15.2 %all-to-all-start.1 = ((f32[8,2,32,360]{3,2,1,0:T(8,128)}), f32[8,2,32,360]{3,2,1,0:T(8,128)S(1)}, u32[]{:S(2)}, u32[]{:S(2)}) async-start(f32[8,2,32,360]{3,2,1,0:T(8,128)} %split.8), calls=%async_computation.1 | async-start | bytes 1572864 | tf_op jit(solution)/shard_map/all_to_all | solution.py:34
  122.6 16.3 %all-to-all-start.2 = ((f32[8,2,40,360]{3,2,1,0:T(8,128)}), f32[8,2,40,360]{3,2,1,0:T(8,128)S(1)}, u32[]{:S(2)}, u32[]{:S(2)}) async-start(f32[8,2,40,360]{3,2,1,0:T(8,128)} %split.9), calls=%async_computation.2 | async-start | bytes 1966080 | tf_op jit(solution)/shard_map/all_to_all | solution.py:34
  126.3 14.9 %copy-start.4 = (bf16[1,72,2880]{2,1,0:T(8,128)(2,1)S(1)}, bf16[1,72,2880]{2,1,0:T(8,128)(2,1)}, u32[]{:S(2)}) copy-start(bf16[1,72,2880]{2,1,0:T(8,128)(2,1)} %copy-done.3) | copy-start | bytes 1244164
  126.3 14.9 %copy-start.6 = (bf16[1,72,2880]{2,1,0:T(8,128)(2,1)S(1)}, bf16[1,72,2880]{2,1,0:T(8,128)(2,1)}, u32[]{:S(2)}) copy-start(bf16[1,72,2880]{2,1,0:T(8,128)(2,1)} %copy-done.5) | copy-start | bytes 1244164
  141.3 14.3 %slice-start.2 = ((s8[5898240]{0:T(1024)(128)(4,1)}), s8[4194304]{0:T(1024)(128)(4,1)S(1)}, s32[]{:S(2)}) async-start(s8[5898240]{0:T(1024)(128)(4,1)} %bitcast.112), calls=%async_computation.8 | async-start | bytes 8388608
  141.3 15.5 %slice-start.4 = ((s8[11796480]{0:T(1024)(128)(4,1)}), s8[4194304]{0:T(1024)(128)(4,1)S(1)}, s32[]{:S(2)}) async-start(s8[11796480]{0:T(1024)(128)(4,1)} %bitcast.121), calls=%async_computation.10 | async-start | bytes 8388608
  143.6 12.0 %slice-start.3 = ((s8[5898240]{0:T(1024)(128)(4,1)}), s8[1703936]{0:T(1024)(128)(4,1)S(1)}, s32[]{:S(2)}) async-start(s8[5898240]{0:T(1024)(128)(4,1)} %bitcast.112), calls=%async_computation.9 | async-start | bytes 3407872
  143.6 13.2 %slice-start.5 = ((s8[11796480]{0:T(1024)(128)(4,1)}), s8[4194304]{0:T(1024)(128)(4,1)S(1)}, s32[]{:S(2)}) async-start(s8[11796480]{0:T(1024)(128)(4,1)} %bitcast.121), calls=%async_computation.11 | async-start | bytes 8388608
  143.6 13.2 %slice-start.6 = ((s8[11796480]{0:T(1024)(128)(4,1)}), s8[3407872]{0:T(1024)(128)(4,1)S(1)}, s32[]{:S(2)}) async-start(s8[11796480]{0:T(1024)(128)(4,1)} %bitcast.121), calls=%async_computation.12 | async-start | bytes 6815744
  155.5 11.7 %copy-start.12 = (bf16[1024,2880]{0,1:T(8,128)(2,1)}, bf16[1024,2880]{0,1:T(8,128)(2,1)S(1)}, u32[]{:S(2)}) copy-start(bf16[1024,2880]{0,1:T(8,128)(2,1)S(1)} %get-tuple-element.76) | copy-start | bytes 17694724
  155.6 13.5 %slice-start = ((s8[5898240]{0:T(1024)(128)(4,1)}), s8[4194304]{0:T(1024)(128)(4,1)S(1)}, s32[]{:S(2)}) async-start(s8[5898240]{0:T(1024)(128)(4,1)} %bitcast.110), calls=%async_computation.6 | async-start | bytes 8388608
  156.8 10.5 %copy-start.8 = (bf16[2,256,2880]{1,2,0:T(8,128)(2,1)S(1)}, bf16[2,256,2880]{1,2,0:T(8,128)(2,1)}, u32[]{:S(2)}) copy-start(bf16[2,256,2880]{1,2,0:T(8,128)(2,1)} %param.9) | copy-start | bytes 8847364
  156.8 12.3 %slice-start.1 = ((s8[5898240]{0:T(1024)(128)(4,1)}), s8[1703936]{0:T(1024)(128)(4,1)S(1)}, s32[]{:S(2)}) async-start(s8[5898240]{0:T(1024)(128)(4,1)} %bitcast.110), calls=%async_computation.7 | async-start | bytes 3407872
  223.9 46.3 %all-to-all-start.5 = ((f32[32,32,329]{2,1,0:T(8,128)}), f32[32,32,329]{2,1,0:T(8,128)S(1)}, u32[]{:S(2)}, u32[]{:S(2)}) async-start(f32[32,32,329]{2,1,0:T(8,128)} %broadcast_in_dim.12), calls=%async_computation.5 | async-start | bytes 3145728 | tf_op jit(solution)/shard_map/all_to_all | solution.py:46
where the time goes:
time: 274 us; the launch traced here: 273 us
  waiting for transfers between devices  66.9 us (24%)
  matrix products  64.1 us (23%)
  other arithmetic  57.3 us (21%)
  blocking collectives  46.4 us (17%)
  starting transfers between devices  20.6 us (8%)
  local copies, waits for them, and re-layouts  16.1 us (6%)
    add x16, other arithmetic, lone_realization(): return (total + slope(values - other.astype(jnp.float32)[None]), None)  48.1 us
    all_to_all x1, blocking collectives, sent_and_summed(): lax.all_to_all(split_up(array, dim, devices), axis, 0, 0, tiled=True)  36.3 us
    all_to_all x1, waiting for transfers between devices, copy_for_each(): lax.all_to_all(jnp.broadcast_to(array[None], (devices, *array.shape)), ax...  28.6 us
    dot_general x2, matrix products, on_device(): jnp.dot(w_out.T, prediction_adjoint, preferred_element_type=jnp.float32)  22.3 us
    dot_general x2, matrix products, on_device(): jnp.dot(w_in, hidden_codes[ensemble_position], preferred_element_type=jnp...  20.1 us
    all_to_all x1, waiting for transfers between devices, on_device(): lax.all_to_all(predicted_maps, 'member', split_axis=2, concat_axis=0, til...  19.4 us
    all_to_all x2, waiting for transfers between devices, exchange_in_pieces(): lax.all_to_all(piece, axis, split_axis=0, concat_axis=0, tiled=True)  18.9 us
    all_to_all x1, blocking collectives, copy_for_each(): lax.all_to_all(jnp.broadcast_to(array[None], (devices, *array.shape)), ax...  10 us
  transfers between devices with their start and end apart: 4, of which 4 were waited for; matrix products, arithmetic and copies ran while one was open for 6% of the time, Pallas kernels for 0%

commit v1 on v0

v1 whole, which is shorter than its diff:
```python
import functools
import math

import jax
import jax.numpy as jnp
from jax import lax
from jax.experimental import pallas as pl
from jax.experimental.pallas import tpu as pltpu
from jax.sharding import PartitionSpec as P

LON = 1440
CHUNK = 384
MESH = pl.DeviceIdType.MESH
K0 = math.sqrt(2.0 / math.pi)
K1 = K0 * 0.044715
F32 = jnp.float32
BF16 = jnp.bfloat16


def kernel(
    geo,
    area_ref, h_ref, w_in_ref, b_in_ref, w_out_ref, b_out_ref, target_ref,
    sens_ref, gin_ref, gout_ref, gb_ref,
    hs, xs, acts, w_in_t, w_out_t, bias, goal, fcast, fpart, ftile, dback,
    acc_in, acc_out, acc_b, gsend, c0, own, p1, c1, z1, c2, fin,
    send_a, recv_a, send_b, recv_b, send_0, recv_0, send_1, recv_1, send_2, recv_2, send_3, recv_3, send_4, recv_4,
):
    n_mem, n_z, cells = geo
    hid, latent = w_in_ref.shape
    chans = w_out_ref.shape[0]
    me = lax.axis_index("member")
    sp = lax.axis_index("space")
    core = lax.rem(sp, 2)
    x_hi = lax.rem(lax.div(sp, 2), 2)
    z = lax.div(sp, 4)
    plane = 2 * n_mem
    my_q = me * 2 + x_hi

    def plane_dev(off):
        q = lax.rem(my_q + off, plane)
        m = lax.div(q, 2)
        s = z * 4 + lax.rem(q, 2) * 2 + core
        return q, {"member": m, "space": s}

    def z_dev(off):
        zz = lax.rem(z + off, n_z)
        return zz, {"space": zz * 4 + x_hi * 2 + core}

    partner = {"space": sp + 1 - 2 * core}

    barrier = pltpu.get_barrier_semaphore()
    for off in range(1, plane):
        pl.semaphore_signal(barrier, inc=1, device_id=plane_dev(off)[1], device_id_type=MESH)
    for off in range(1, n_z):
        pl.semaphore_signal(barrier, inc=1, device_id=z_dev(off)[1], device_id_type=MESH)
    pl.semaphore_signal(barrier, inc=1, device_id=partner, device_id_type=MESH)

    full = cells // CHUNK
    rest = cells - full * CHUNK
    for c in range(n_mem):
        for m in range(2):
            if c < full:
                hs[c, :, m * CHUNK:(m + 1) * CHUNK] = h_ref[m, :, c * CHUNK:(c + 1) * CHUNK]
            else:
                hs[c, :, m * CHUNK:(m + 1) * CHUNK] = jnp.concatenate(
                    [h_ref[m, :, c * CHUNK:cells], jnp.zeros((latent, CHUNK - rest), BF16)], axis=1)
        if c < full:
            goal[c] = target_ref[:, c * CHUNK:(c + 1) * CHUNK].astype(F32)
        else:
            goal[c] = jnp.concatenate(
                [target_ref[:, c * CHUNK:cells].astype(F32), jnp.zeros((chans, CHUNK - rest), F32)], axis=1)
    w_in_t[...] = w_in_ref[...].T
    w_out_t[...] = w_out_ref[...].T
    bias[...] = jnp.broadcast_to(b_in_ref[...], (hid, 128))
    acc_in[...] = jnp.zeros_like(acc_in)
    acc_out[...] = jnp.zeros_like(acc_out)
    acc_b[...] = jnp.zeros_like(acc_b)

    pl.semaphore_wait(barrier, plane - 1 + n_z - 1 + 1)

    def a_copy(d, slot):
        return pltpu.make_async_remote_copy(
            src_ref=fcast.at[d], dst_ref=fpart.at[slot], send_sem=send_a.at[d], recv_sem=recv_a.at[slot],
            device_id={"member": d}, device_id_type=MESH)

    def b_copy(d, slot):
        return pltpu.make_async_remote_copy(
            src_ref=fpart.at[d], dst_ref=dback.at[slot], send_sem=send_b.at[d], recv_sem=recv_b.at[slot],
            device_id={"member": d}, device_id_type=MESH)

    def forward(step, carry):
        c = lax.rem(me + 1 + step, n_mem)
        for j in range(2 * CHUNK // 256):
            cols = slice(j * 256, (j + 1) * 256)
            pre = jnp.dot(w_in_ref[...], hs[c, :, cols], preferred_element_type=F32)
            b2 = bias[...]
            x = pre + jnp.concatenate([b2, b2], axis=1)
            xs[c, :, cols] = x
            t = jnp.tanh(x * (K0 + K1 * (x * x)))
            acts[c, :, cols] = (x * (0.5 * t + 0.5)).astype(BF16)
        out = jnp.dot(w_out_ref[...], acts[c], preferred_element_type=F32) + b_out_ref[...]
        fcast[c] = out.astype(BF16)

        @pl.when(step < n_mem - 1)
        def _():
            a_copy(c, me).start()

        return carry

    lax.fori_loop(0, n_mem, forward, 0)
    fpart[me] = fcast[me]
    for off in range(1, n_mem):
        p = lax.rem(me + n_mem - off, n_mem)
        a_copy(p, p).wait_recv()
    for p in range(n_mem):
        for m in range(2):
            ftile[2 * p + m] = fpart[p, :, m * CHUNK:(m + 1) * CHUNK].astype(F32)

    lanes = lax.broadcasted_iota(jnp.int32, (8, 128), 1)

    def pairs(r, carry):
        rows = pl.ds(pl.multiple_of(r * 8, 8), 8)
        for k in range(CHUNK // 128):
            cols = slice(k * 128, (k + 1) * 128)
            cell = me * CHUNK + k * 128 + lanes
            area = jnp.where(cell < LON, area_ref[0], jnp.where(cell < 2 * LON, area_ref[1], 0.0))
            f = [ftile[i, rows, cols] for i in range(2 * n_mem)]
            total = [None] * (2 * n_mem)
            for i in range(2 * n_mem):
                for j in range(i + 1, 2 * n_mem):
                    d = f[i] - f[j]
                    v = d * lax.rsqrt(d * d + 0.0625)
                    total[i] = v if total[i] is None else total[i] + v
                    total[j] = -v if total[j] is None else total[j] - v
            g = goal[me, rows, cols]
            for i in range(2 * n_mem):
                d = f[i] - g
                v = d * lax.rsqrt(d * d + 0.0625)
                ftile[i, rows, cols] = area * (v - total[i] * (1.0 / (2 * n_mem)))
        return carry

    lax.fori_loop(0, chans // 8, pairs, 0)
    for p in range(n_mem):
        for m in range(2):
            fpart[p, :, m * CHUNK:(m + 1) * CHUNK] = ftile[2 * p + m].astype(BF16)
    for off in range(1, n_mem):
        d = lax.rem(me + off, n_mem)
        b_copy(d, me).start()
    dback[me] = fpart[me]

    def backward(step, carry):
        c = lax.rem(me + n_mem - step, n_mem)

        @pl.when(step > 0)
        def _():
            b_copy(c, c).wait_recv()

        d = dback[c]
        acc_out[:, :chans] += lax.dot_general(
            acts[c], d, (((1,), (1,)), ((), ())), preferred_element_type=F32)
        for j in range(2 * CHUNK // 256):
            cols = slice(j * 256, (j + 1) * 256)
            dact = jnp.dot(w_out_t[...], d[:, cols], preferred_element_type=F32)
            x = xs[c, :, cols]
            x2 = x * x
            t = jnp.tanh(x * (K0 + K1 * x2))
            s = 0.5 * t + 0.5
            slope = s * (1.0 + (x * (1.0 - s)) * (2 * K0 + (6 * K1) * x2))
            dpre = (dact * slope).astype(BF16)
            acts[c, :, cols] = dpre
            wide = dpre.astype(F32)
            acc_b[...] += wide[:, :128] + wide[:, 128:]
        acc_in[...] += lax.dot_general(
            acts[c], hs[c], (((1,), (1,)), ((), ())), preferred_element_type=F32)
        return carry

    lax.fori_loop(0, n_mem, backward, 0)

    def sens_of(c):
        out = jnp.dot(w_in_t[...], acts[c], preferred_element_type=F32).astype(BF16)
        for m in range(2):
            size = CHUNK if c < full else rest
            sens_ref[m, :, c * CHUNK:c * CHUNK + size] = out[:, m * CHUNK:m * CHUNK + size]

    half = hid // 2
    share = half // plane
    lane = lax.broadcasted_iota(jnp.int32, (hid, 128), 1)
    summed_b = jnp.sum(acc_b[...], axis=1, keepdims=True)
    acc_out[...] = jnp.where(lane == chans, summed_b, acc_out[...])
    theirs = pl.ds(pl.multiple_of((1 - core) * half, half), half)
    mine = pl.ds(pl.multiple_of(core * half, half), half)
    gsend[:, :latent] = acc_in[theirs, :].astype(BF16)
    gsend[:, latent:] = acc_out[theirs, :].astype(BF16)
    copy0 = pltpu.make_async_remote_copy(
        src_ref=gsend, dst_ref=c0, send_sem=send_0.at[0], recv_sem=recv_0.at[0], device_id=partner, device_id_type=MESH)
    copy0.start()
    sens_of(0)
    copy0.wait_recv()
    own[:, :latent] = acc_in[mine, :] + c0[:, :latent].astype(F32)
    own[:, latent:] = acc_out[mine, :] + c0[:, latent:].astype(F32)
    for q in range(plane):
        p1[q] = own[q * share:(q + 1) * share, :].astype(BF16)

    def one_copy(q, slot, dev):
        return pltpu.make_async_remote_copy(
            src_ref=p1.at[q], dst_ref=c1.at[slot], send_sem=send_1.at[q], recv_sem=recv_1.at[slot],
            device_id=dev, device_id_type=MESH)

    for off in range(1, plane):
        q, dev = plane_dev(off)
        one_copy(q, my_q, dev).start()
    c1[my_q] = p1[my_q]
    for c in range(1, 4):
        sens_of(c)
    for off in range(1, plane):
        q, dev = plane_dev(plane - off)
        one_copy(q, q, dev).wait_recv()
    part = c1[0].astype(F32)
    for q in range(1, plane):
        part = part + c1[q].astype(F32)
    z1[...] = part.astype(BF16)

    def two_copy(zz, slot, dev):
        return pltpu.make_async_remote_copy(
            src_ref=z1, dst_ref=c2.at[slot], send_sem=send_2.at[zz], recv_sem=recv_2.at[slot],
            device_id=dev, device_id_type=MESH)

    for off in (4, 3, 5, 2, 6, 1, 7):
        zz, dev = z_dev(off)
        two_copy(zz, z, dev).start()
    c2[z] = z1[...]
    for c in range(4, 7):
        sens_of(c)
    for off in range(1, n_z):
        zz, dev = z_dev(off)
        two_copy(zz, zz, dev).wait_recv()
    part = c2[0].astype(F32)
    for zz in range(1, n_z):
        part = part + c2[zz].astype(F32)
    slot = core * plane + my_q
    fin[slot] = part.astype(BF16)

    def three_copy(src_q, dst_q, dev):
        return pltpu.make_async_remote_copy(
            src_ref=fin.at[slot], dst_ref=fin.at[core * plane + src_q], send_sem=send_3.at[dst_q],
            recv_sem=recv_3.at[src_q], device_id=dev, device_id_type=MESH)

    def four_copy(q, c):
        return pltpu.make_async_remote_copy(
            src_ref=fin.at[c * plane + q], dst_ref=fin.at[c * plane + q], send_sem=send_4.at[q],
            recv_sem=recv_4.at[q], device_id=partner, device_id_type=MESH)

    for off in range(1, plane):
        q, dev = plane_dev(off)
        three_copy(my_q, q, dev).start()
    four_copy(my_q, core).start()
    sens_of(7)
    for off in range(1, plane):
        q, dev = plane_dev(plane - off)
        three_copy(q, q, dev).wait_recv()
        four_copy(q, core).start()
    for q in range(plane):
        four_copy(q, 1 - core).wait_recv()

    scale = 1.0 / math.sqrt(2 * n_mem * cells)
    for r in range(2 * plane):
        rows = slice(r * share, (r + 1) * share)
        gin_ref[rows, :] = fin[r, :, :latent].astype(F32) * scale
        acc_out[rows, :] = fin[r, :, latent:].astype(F32) * scale
    flipped = acc_out[...].T
    gout_ref[...] = flipped[:chans, :]
    gb_ref[...] = flipped[chans:chans + 1, :]

    for off in range(1, n_mem):
        d = lax.rem(me + off, n_mem)
        a_copy(d, me).wait_send()
        b_copy(d, me).wait_send()
    copy0.wait_send()
    for off in range(1, plane):
        q, dev = plane_dev(off)
        one_copy(q, my_q, dev).wait_send()
        three_copy(my_q, q, dev).wait_send()
    for off in range(1, n_z):
        zz, dev = z_dev(off)
        two_copy(zz, z, dev).wait_send()
    for q in range(plane):
        four_copy(q, core).wait_send()


def on_device(hidden_codes, w_in, b_in, w_out, b_out, target, band_start):
    mem, latent, cells = hidden_codes.shape
    hid = w_in.shape[0]
    chans = w_out.shape[0]
    rows = cells // LON
    n_mem = lax.axis_size("member")
    n_space = lax.axis_size("space")
    n_z = n_space // 4
    plane = 2 * n_mem
    angle = ((band_start[0] + jnp.arange(rows, dtype=jnp.int32)).astype(F32) + 0.5) * (
        math.pi / (rows * n_space)) - math.pi / 2
    area = jnp.cos(angle)
    wide = latent + 128
    half = hid // 2
    share = half // plane
    vm = pl.BlockSpec(memory_space=pltpu.VMEM)
    dma = pltpu.SemaphoreType.DMA
    sens, gin, gout, gb = pl.pallas_call(
        functools.partial(kernel, (n_mem, n_z, cells)),
        out_shape=(
            jax.ShapeDtypeStruct(hidden_codes.shape, BF16),
            jax.ShapeDtypeStruct((hid, latent), F32),
            jax.ShapeDtypeStruct((chans, hid), F32),
            jax.ShapeDtypeStruct((1, hid), F32),
        ),
        in_specs=[pl.BlockSpec(memory_space=pltpu.SMEM)] + [vm] * 6,
        out_specs=(vm, vm, vm, vm),
        scratch_shapes=[
            pltpu.VMEM((n_mem, latent, 2 * CHUNK), BF16),
            pltpu.VMEM((n_mem, hid, 2 * CHUNK), F32),
            pltpu.VMEM((n_mem, hid, 2 * CHUNK), BF16),
            pltpu.VMEM((latent, hid), BF16),
            pltpu.VMEM((hid, chans), BF16),
            pltpu.VMEM((hid, 128), F32),
            pltpu.VMEM((n_mem, chans, CHUNK), F32),
            pltpu.VMEM((n_mem, chans, 2 * CHUNK), BF16),
            pltpu.VMEM((n_mem, chans, 2 * CHUNK), BF16),
            pltpu.VMEM((2 * n_mem, chans, CHUNK), F32),
            pltpu.VMEM((n_mem, chans, 2 * CHUNK), BF16),
            pltpu.VMEM((hid, latent), F32),
            pltpu.VMEM((hid, 128), F32),
            pltpu.VMEM((hid, 128), F32),
            pltpu.VMEM((half, wide), BF16),
            pltpu.VMEM((half, wide), BF16),
            pltpu.VMEM((half, wide), F32),
            pltpu.VMEM((plane, share, wide), BF16),
            pltpu.VMEM((plane, share, wide), BF16),
            pltpu.VMEM((share, wide), BF16),
            pltpu.VMEM((n_z, share, wide), BF16),
            pltpu.VMEM((2 * plane, share, wide), BF16),
            dma((n_mem,)), dma((n_mem,)), dma((n_mem,)), dma((n_mem,)),
            dma((1,)), dma((1,)), dma((plane,)), dma((plane,)), dma((n_z,)), dma((n_z,)),
            dma((plane,)), dma((plane,)), dma((plane,)), dma((plane,)),
        ],
        compiler_params=pltpu.CompilerParams(
            collective_id=0, has_side_effects=True, vmem_limit_bytes=67043328),
    )(area, hidden_codes, w_in, b_in.reshape(hid, 1), w_out, b_out.reshape(chans, 1), target)
    return sens, gin, gout, gb.reshape(hid)


def solution(mesh):
    in_specs = (P("member", None, "space"), P(), P(), P(), P(), P(None, "space"), P("space"))
    out_specs = (P("member", None, "space"), P(), P(), P())
    return jax.shard_map(
        on_device, mesh=mesh, in_specs=in_specs, out_specs=out_specs, check_vma=False
    )
```

time: 274 us -> 107 us (0.39)
  Pallas kernels: 0 us -> 89.8 us
  waiting for transfers between devices: 66.9 us -> 0 us
  matrix products: 64.1 us -> 0 us
  other arithmetic: 57.3 us -> 0.56 us
  blocking collectives: 46.4 us -> 0 us
  starting transfers between devices: 20.6 us -> 0 us
    pallas_call x0 -> x1, Pallas kernels: none -> 89.8 us  [on_device(): pl.pallas_call(functools.partial(kernel, (n_mem, n_z, cells)), out_shape=...]
    all_to_all x4 -> x0, waiting for transfers between devices: 66.9 us -> none  [the longest x1 28.6 us: copy_for_each(): lax.all_to_all(jnp.broadcast_to(array[None], (devices, *array.shape)), ax...]
    dot_general x12 -> x0, matrix products: 64.1 us -> none  [the longest x2 22.3 us: on_device(): jnp.dot(w_out.T, prediction_adjoint, preferred_element_type=jnp.float32)]
    add x16 -> x0, other arithmetic: 48.1 us -> none  [lone_realization(): return (total + slope(values - other.astype(jnp.float32)[None]), None)]
    all_to_all x2 -> x0, blocking collectives: 46.4 us -> none  [the longest x1 36.3 us: sent_and_summed(): lax.all_to_all(split_up(array, dim, devices), axis, 0, 0, tiled=True)]
    all_to_all x4 -> x0, starting transfers between devices: 20.6 us -> none  [the longest x2 7.48 us: exchange_in_pieces(): lax.all_to_all(piece, axis, split_axis=0, concat_axis=0, tiled=True)]
    unnamed x41 -> x11, local copies, waits for them, and re-layouts: 3.26 us -> 11.5 us
    convert_element_type x3 -> x0, other arithmetic: 4.54 us -> none  [the longest x1 2.3 us: on_device(): prediction_sensitivity = (area[None, None, :] * (slope(diagonal_contribut...]
  transfers between devices with their start and end apart: 4 -> 0, of which waited for: 4 -> 0; matrix products, arithmetic and copies ran while one was open for 6% -> 0% of each run, Pallas kernels for 0% -> 0%
where the time goes in v1:
time: 107 us; the launch traced here: 106 us
  Pallas kernels  89.8 us (84%)
  local copies, waits for them, and re-layouts  14.6 us (14%)
  between operations  1.31 us (1%)
    pallas_call x1, Pallas kernels, on_device(): pl.pallas_call(functools.partial(kernel, (n_mem, n_z, cells)), out_shape=...  89.8 us
    unnamed x11, local copies, waits for them, and re-layouts  11.5 us

profile of v1, /device:TPU:1, one launch (start us, length us, event | category | flops | bytes accessed | tf_op | source)
XLA Modules:
  0.0 106.3 jit_solution(16668037901747223892)
XLA Ops:
  1.3 0.6 add_cosine_fusion.area_ref
  1.8 1.4 %copy.16.b_out_ref = f32[72,1]{1,0:T(8,128)} copy(f32[72,1]{0,1:T(1,128)} %bitcast.7) | data formatting | bytes 576 | tf_op jit(solution)/shard_map/reshape | solution.py:346
  3.2 1.7 %copy.15.b_in_ref = f32[1024,1]{1,0:T(8,128)} copy(f32[1024,1]{0,1:T(1,128)} %bitcast.5) | data formatting | bytes 8192 | tf_op jit(solution)/shard_map/reshape | solution.py:346
  4.9 4.6 %copy.14.h_ref = bf16[2,256,2880]{2,1,0:T(8,128)(2,1)} copy(bf16[2,256,2880]{1,2,0:T(8,128)(2,1)} %param.7) | data formatting | bytes 5898240 | tf_op args[0]
  9.5 89.8 %shard_map.102 = (bf16[2,256,2880]{2,1,0:T(8,128)(2,1)}, f32[1024,256]{1,0:T(8,128)}, f32[72,1024]{1,0:T(8,128)}, f32[1,1024]{1,0:T(1,128)}) custom-call(f32[2]{0:T(128)} %add_cosine_fusion.area_ref, bf16[2,256,2880]{2,1,0:T(8,128)(2,1)} %copy.14.h_ref, bf16[1024,256]{1,0:T(8,128)(2,1)} %w_in_ref.1, f32[1024,1]{1,0:T(8,128)} %copy.15.b_in_ref, ...), custom_call_target="tpu_custom_call" | custom-call | tf_op jit(solution)/shard_map/pallas_call | solution.py:307
  99.3 0.0 copy-start
  99.3 0.0 copy-start.1
  99.3 0.0 copy-start.2
  99.3 4.7 %copy.17 = bf16[2,256,2880]{1,2,0:T(8,128)(2,1)} copy(bf16[2,256,2880]{2,1,0:T(8,128)(2,1)} %get-tuple-element.16) | data formatting | bytes 5898240
  104.0 0.0 copy-done
  104.0 1.0 copy.22
  105.0 0.0 copy-done.1
  105.0 0.7 copy.23
  105.7 0.0 copy-done.2
  105.7 0.6 copy.24
Async XLA Ops:
  99.3 4.7 %copy-start = (f32[1024,256]{1,0:T(8,128)S(1)}, f32[1024,256]{1,0:T(8,128)}, u32[]{:S(2)}) copy-start(f32[1024,256]{1,0:T(8,128)} %get-tuple-element.25) | copy-start | bytes 3145732
  99.3 5.7 %copy-start.1 = (f32[72,1024]{1,0:T(8,128)S(1)}, f32[72,1024]{1,0:T(8,128)}, u32[]{:S(2)}) copy-start(f32[72,1024]{1,0:T(8,128)} %get-tuple-element.26) | copy-start | bytes 884740
  99.3 6.4 %copy-start.2 = (f32[1,1024]{1,0:T(1,128)S(1)}, f32[1,1024]{1,0:T(1,128)}, u32[]{:S(2)}) copy-start(f32[1,1024]{1,0:T(1,128)} %get-tuple-element.11) | copy-start | bytes 12292

commit v2 on v0

v2 whole, which is shorter than its diff:
```python
import functools
import math

import jax
import jax.numpy as jnp
from jax import lax
from jax.experimental import pallas as pl
from jax.experimental.pallas import tpu as pltpu
from jax.sharding import PartitionSpec as P

LON = 1440
SUBS = (256, 128)
CHUNK = sum(SUBS)
PARTS = 2
LATE = 2
MESH = pl.DeviceIdType.MESH
K0 = math.sqrt(2.0 / math.pi)
K1 = K0 * 0.044715
F32 = jnp.float32
BF16 = jnp.bfloat16


class Mark:
    def __init__(self):
        self.cm = None

    def __call__(self, name):
        if self.cm is not None:
            self.cm.__exit__(None, None, None)
            self.cm = None
        if name:
            self.cm = jax.named_scope(name)
            self.cm.__enter__()


def kernel(
    geo,
    area_ref, h_ref, w_in_hbm, b_in_hbm, w_out_hbm, b_out_hbm, target_hbm,
    sens_ref, fin_ref,
    w_in_ref, b_in_ref, w_out_ref, b_out_ref, target_ref,
    hs0, hs1, slopes0, slopes1, acts0, acts1, fcast0, fcast1, fpart0, fpart1, dback0, dback1,
    w_half, w_in_t, w_out_t, bias, bias_out, goal, ftile,
    acc_in, acc_out, acc_b, gsend, c0, own, p1, c1, z1, c2, fin,
    send_a, recv_a, send_b, recv_b, send_0, recv_0, send_1, recv_1, send_2, recv_2, send_3, recv_3, send_4, recv_4,
    load, store, keep, given,
):
    n_mem, n_z, cells = geo
    hid, latent = w_in_hbm.shape
    chans = w_out_hbm.shape[0]
    hs, slopes, acts = (hs0, hs1), (slopes0, slopes1), (acts0, acts1)
    fcast, fpart, dback = (fcast0, fcast1), (fpart0, fpart1), (dback0, dback1)
    me = lax.axis_index("member")
    sp = lax.axis_index("space")
    core = lax.rem(sp, 2)
    x_hi = lax.rem(lax.div(sp, 2), 2)
    z = lax.div(sp, 4)
    plane = 2 * n_mem
    my_q = me * 2 + x_hi
    full = cells // CHUNK
    rest = cells - full * CHUNK
    first_at = (0, SUBS[0])

    def plane_dev(off):
        q = lax.rem(my_q + off, plane)
        return q, {"member": lax.div(q, 2), "space": z * 4 + lax.rem(q, 2) * 2 + core}

    def z_dev(off):
        zz = lax.rem(z + off, n_z)
        return zz, {"space": zz * 4 + x_hi * 2 + core}

    partner = {"space": sp + 1 - 2 * core}
    mark = Mark()
    mark('entry')

    weights = [
        pltpu.make_async_copy(far, near, given.at[i]) for i, (far, near) in enumerate((
            (w_in_hbm, w_in_ref), (w_out_hbm, w_out_ref), (b_in_hbm, b_in_ref), (b_out_hbm, b_out_ref),
            (target_hbm, target_ref)))]
    for copy in weights:
        copy.start()

    def pieces(c, b, size):
        return [(m, pl.ds(c * CHUNK + first_at[b], size), pl.ds(m * SUBS[b], size)) for m in range(2)]

    def load_copies(c, b, size):
        return [
            pltpu.make_async_copy(h_ref.at[m, far, :], hs[b].at[c, near, :], load.at[b * n_mem + c])
            for m, far, near in pieces(c, b, size)]

    def store_copies(c, b, size):
        return [
            pltpu.make_async_copy(hs[b].at[c, near, :], sens_ref.at[m, far, :], store.at[0])
            for m, far, near in pieces(c, b, size)]

    def load_wait(c, b, size):
        pltpu.make_async_copy(
            h_ref.at[0, pl.ds(0, 2 * size), :], hs[b].at[c, pl.ds(0, 2 * size), :], load.at[b * n_mem + c]).wait()

    all_pieces = [(c, 0, SUBS[0] if c < full else rest) for c in range(n_mem)] + [(c, 1, SUBS[1]) for c in range(full)]
    for piece in all_pieces:
        for copy in load_copies(*piece):
            copy.start()

    barrier = pltpu.get_barrier_semaphore()
    for off in range(1, plane):
        pl.semaphore_signal(barrier, inc=1, device_id=plane_dev(off)[1], device_id_type=MESH)
    for off in range(1, n_z):
        pl.semaphore_signal(barrier, inc=1, device_id=z_dev(off)[1], device_id_type=MESH)
    pl.semaphore_signal(barrier, inc=1, device_id=partner, device_id_type=MESH)

    mark('prep')
    for copy in weights:
        copy.wait()
    for m in range(2):
        hs0[full, m * SUBS[0] + rest:(m + 1) * SUBS[0], :] = jnp.zeros((SUBS[0] - rest, latent), BF16)
    for c in range(n_mem):
        if c < full:
            goal[c] = target_ref[:, c * CHUNK:(c + 1) * CHUNK].astype(F32)
        else:
            goal[c] = jnp.concatenate(
                [target_ref[:, c * CHUNK:cells].astype(F32), jnp.zeros((chans, CHUNK - rest), F32)], axis=1)
    w_in_t[...] = w_in_ref[...].T
    w_half[...] = w_in_ref[...] * 0.5
    w_out_t[...] = w_out_ref[...].T * 0.5
    bias[...] = jnp.broadcast_to(0.5 * b_in_ref[...], (128, hid)).T
    bias_out[...] = jnp.broadcast_to(b_out_ref[...], (128, chans)).T
    acc_in[...] = jnp.zeros_like(acc_in)
    acc_out[...] = jnp.zeros_like(acc_out)
    acc_b[...] = jnp.zeros_like(acc_b)

    def a_copy(b, d, slot):
        return pltpu.make_async_remote_copy(
            src_ref=fcast[b].at[d], dst_ref=fpart[b].at[slot], send_sem=send_a.at[b],
            recv_sem=recv_a.at[b], device_id={"member": d}, device_id_type=MESH)

    def b_copy(b, d, slot):
        return pltpu.make_async_remote_copy(
            src_ref=fpart[b].at[d], dst_ref=dback[b].at[slot], send_sem=send_b.at[b],
            recv_sem=recv_b.at[b * n_mem + slot], device_id={"member": d}, device_id_type=MESH)

    def took(ref, sem):
        pltpu.make_async_copy(ref, ref, sem).wait()

    def forward_chunk(b, c):
        b2 = jnp.concatenate([bias[...]] * 2, axis=1)
        bo2 = jnp.concatenate([bias_out[...]] * 2, axis=1)
        for j in range(2 * SUBS[b] // 256):
            cols = slice(j * 256, (j + 1) * 256)
            x = lax.dot_general(
                w_half[...], hs[b][c, cols, :], (((1,), (1,)), ((), ())), preferred_element_type=F32) + b2
            poly = 2.0 * K0 + (8.0 * K1) * (x * x)
            t = jnp.tanh(x * poly)
            p = 1.0 + t
            a = x * p
            slopes[b][c, :, cols] = p + (a * (1.0 - t)) * (3.0 * poly - 4.0 * K0)
            a = a.astype(BF16)
            acts[b][c, :, cols] = a
            fcast[b][c, :, cols] = (jnp.dot(w_out_ref[...], a, preferred_element_type=F32) + bo2).astype(BF16)

    mark('forward0')

    def forward0(step, carry):
        c = lax.rem(me + 1 + step, n_mem)

        @pl.when(c < full)
        def _():
            load_wait(c, 0, SUBS[0])

        @pl.when(c == full)
        def _():
            load_wait(c, 0, rest)

        forward_chunk(0, c)

        @pl.when(step == LATE)
        def _():
            pl.semaphore_wait(barrier, plane - 1 + n_z - 1 + 1)
            for early in range(LATE):
                a_copy(0, lax.rem(me + 1 + early, n_mem), me).start()

        @pl.when((step >= LATE) & (step < n_mem - 1))
        def _():
            a_copy(0, c, me).start()

        return carry

    lax.fori_loop(0, n_mem, forward0, 0)
    mark('forward1')

    def forward1(step, carry):
        c = lax.rem(me + 1 + step, n_mem)

        @pl.when(c < full)
        def _():
            load_wait(c, 1, SUBS[1])
            forward_chunk(1, c)

            @pl.when(step < n_mem - 1)
            def _():
                a_copy(1, c, me).start()

        return carry

    lax.fori_loop(0, n_mem, forward1, 0)

    lanes = lax.broadcasted_iota(jnp.int32, (8, 128), 1)

    def meet(b):
        size = SUBS[b]
        at = first_at[b]
        fpart[b][me] = fcast[b][me]
        took(fpart[b].at[pl.ds(0, n_mem - 1)], recv_a.at[b])
        mark(f'pairs{b}')
        for p in range(n_mem):
            for m in range(2):
                ftile[2 * p + m, :, at:at + size] = fpart[b][p, :, m * size:(m + 1) * size].astype(F32)

        def pairs(r, carry):
            rows = pl.ds(pl.multiple_of(r * 8, 8), 8)
            for k in range(size // 128):
                cols = slice(at + k * 128, at + (k + 1) * 128)
                cell = me * CHUNK + (at + k * 128) + lanes
                area = jnp.where(cell < LON, area_ref[0], jnp.where(cell < 2 * LON, area_ref[1], 0.0))
                f = [ftile[i, rows, cols] for i in range(2 * n_mem)]
                total = [None] * (2 * n_mem)
                for i in range(2 * n_mem):
                    for j in range(i + 1, 2 * n_mem):
                        d = f[i] - f[j]
                        v = d * lax.rsqrt(d * d + 0.0625)
                        total[i] = v if total[i] is None else total[i] + v
                        total[j] = -v if total[j] is None else total[j] - v
                g = goal[me, rows, cols]
                for i in range(2 * n_mem):
                    d = f[i] - g
                    v = d * lax.rsqrt(d * d + 0.0625)
                    ftile[i, rows, cols] = area * (v - total[i] * (1.0 / (2 * n_mem)))
            return carry

        lax.fori_loop(0, chans // 8, pairs, 0)
        for p in range(n_mem):
            for m in range(2):
                fpart[b][p, :, m * size:(m + 1) * size] = ftile[2 * p + m, :, at:at + size].astype(BF16)
        for off in range(1, n_mem):
            d = lax.rem(me + off, n_mem)
            b_copy(b, d, me).start()
        dback[b][me] = fpart[b][me]

    mark('waitA0')
    meet(0)
    mark('waitA1')

    @pl.when(me < full)
    def _():
        meet(1)

    def backward_chunk(b, c):
        d = dback[b][c]
        acc_out[:, :chans] += lax.dot_general(
            acts[b][c], d, (((1,), (1,)), ((), ())), preferred_element_type=F32)
        for j in range(2 * SUBS[b] // 256):
            cols = slice(j * 256, (j + 1) * 256)
            dact = jnp.dot(w_out_t[...], d[:, cols], preferred_element_type=F32)
            dpre = (dact * slopes[b][c, :, cols]).astype(BF16)
            acts[b][c, :, cols] = dpre
            wide = dpre.astype(F32)
            acc_b[...] += wide[:, :128] + wide[:, 128:]
        acc_in[...] += jnp.dot(acts[b][c], hs[b][c], preferred_element_type=F32)

    def backward0(step, carry):
        c = lax.rem(me + n_mem - step, n_mem)

        @pl.when(step > 0)
        def _():
            b_copy(0, c, c).wait_recv()

        backward_chunk(0, c)
        return carry

    def backward1(step, carry):
        c = lax.rem(me + n_mem - step, n_mem)

        @pl.when(c < full)
        def _():
            @pl.when(step > 0)
            def _():
                b_copy(1, c, c).wait_recv()

            backward_chunk(1, c)

        return carry

    mark('backward0')
    lax.fori_loop(0, n_mem, backward0, 0)
    mark('backward1')
    lax.fori_loop(0, n_mem, backward1, 0)

    def sens_of(*chunks):
        for c in chunks:
            for piece in all_pieces:
                if piece[0] == c:
                    b = piece[1]
                    hs[b][c] = jnp.dot(w_in_t[...], acts[b][c], preferred_element_type=F32).T.astype(BF16)
                    for copy in store_copies(*piece):
                        copy.start()

    mark('gradprep')
    half = hid // 2
    block = half // PARTS
    share = block // plane
    lane = lax.broadcasted_iota(jnp.int32, (hid, 128), 1)
    summed_b = jnp.sum(acc_b[...], axis=1, keepdims=True)
    acc_out[...] = jnp.where(lane == chans, summed_b, acc_out[...])

    def zero_copy(r):
        return pltpu.make_async_remote_copy(
            src_ref=gsend.at[r], dst_ref=c0.at[r], send_sem=send_0.at[r], recv_sem=recv_0.at[r],
            device_id=partner, device_id_type=MESH)

    def one_copy(r, q, slot, dev):
        return pltpu.make_async_remote_copy(
            src_ref=p1.at[r, q], dst_ref=c1.at[r, slot], send_sem=send_1.at[r],
            recv_sem=recv_1.at[r], device_id=dev, device_id_type=MESH)

    def two_copy(r, zz, slot, dev):
        return pltpu.make_async_remote_copy(
            src_ref=z1.at[r], dst_ref=c2.at[r, slot], send_sem=send_2.at[r],
            recv_sem=recv_2.at[r], device_id=dev, device_id_type=MESH)

    def at_fin(r, k, q):
        return (k * PARTS + r) * plane + q

    def three_copy(r, src_q, dst_q, dev):
        return pltpu.make_async_remote_copy(
            src_ref=fin.at[at_fin(r, core, my_q)], dst_ref=fin.at[at_fin(r, core, src_q)],
            send_sem=send_3.at[r], recv_sem=recv_3.at[r],
            device_id=dev, device_id_type=MESH)

    def of_core(r, k):
        return pl.ds(at_fin(r, k, 0), plane)

    def four_copy(r):
        mine = fin.at[of_core(r, core)]
        return pltpu.make_async_remote_copy(
            src_ref=mine, dst_ref=mine, send_sem=send_4.at[r], recv_sem=recv_4.at[r],
            device_id=partner, device_id_type=MESH)

    def fin_out(r, k):
        return pltpu.make_async_copy(fin.at[of_core(r, k)], fin_ref.at[of_core(r, k)], keep.at[0])

    for r in range(PARTS):
        theirs = pl.ds(pl.multiple_of((1 - core) * half + r * block, block), block)
        gsend[r, :, :latent] = acc_in[theirs, :].astype(BF16)
        gsend[r, :, latent:] = acc_out[theirs, :].astype(BF16)
        zero_copy(r).start()
    mark('sens0')
    sens_of(0)
    for r in range(PARTS):
        mark(f'wait0.{r}')
        zero_copy(r).wait_recv()
        mark(f'sum0.{r}')
        mine = pl.ds(pl.multiple_of(core * half + r * block, block), block)
        own[:, :latent] = acc_in[mine, :] + c0[r, :, :latent].astype(F32)
        own[:, latent:] = acc_out[mine, :] + c0[r, :, latent:].astype(F32)
        for q in range(plane):
            p1[r, q] = own[q * share:(q + 1) * share, :].astype(BF16)
        for off in range(1, plane):
            q, dev = plane_dev(off)
            one_copy(r, q, my_q, dev).start()
        c1[r, my_q] = p1[r, my_q]
    mark('sens1')
    sens_of(1, 2, 3)
    for r in range(PARTS):
        mark(f'wait1.{r}')
        took(c1.at[r, pl.ds(0, plane - 1)], recv_1.at[r])
        mark(f'sum1.{r}')
        part = c1[r, 0].astype(F32)
        for q in range(1, plane):
            part = part + c1[r, q].astype(F32)
        z1[r] = part.astype(BF16)
        for off in (4, 3, 5, 2, 6, 1, 7):
            zz, dev = z_dev(off)
            two_copy(r, zz, z, dev).start()
        c2[r, z] = z1[r]
        mark(f'sens2.{r}')
        if r == 0:
            sens_of(4, 5)
        if r == PARTS - 1:
            sens_of(6)
    for r in range(PARTS):
        mark(f'wait2.{r}')
        took(c2.at[r, pl.ds(0, n_z - 1)], recv_2.at[r])
        mark(f'sum2.{r}')
        part = c2[r, 0].astype(F32)
        for zz in range(1, n_z):
            part = part + c2[r, zz].astype(F32)
        fin[at_fin(r, core, my_q)] = part.astype(BF16)
        for off in range(1, plane):
            q, dev = plane_dev(off)
            three_copy(r, my_q, q, dev).start()
        if r == 0:
            sens_of(7)
    for r in range(PARTS):
        mark(f'wait3.{r}')
        took(fin.at[pl.ds(0, plane - 1)], recv_3.at[r])
        four_copy(r).start()
        fin_out(r, core).start()
    for r in range(PARTS):
        mark(f'wait4.{r}')
        took(fin.at[pl.ds(0, plane)], recv_4.at[r])
        fin_out(r, 1 - core).start()
    mark('drain')
    took(sens_ref, store.at[0])
    took(fcast[0].at[pl.ds(0, n_mem - 1)], send_a.at[0])
    took(fpart[0].at[pl.ds(0, n_mem - 1)], send_b.at[0])

    @pl.when(me < full)
    def _():
        took(fcast[1].at[pl.ds(0, full - 1)], send_a.at[1])
        took(fpart[1].at[pl.ds(0, n_mem - 1)], send_b.at[1])

    @pl.when(me == full)
    def _():
        took(fcast[1].at[pl.ds(0, full)], send_a.at[1])

    for r in range(PARTS):
        zero_copy(r).wait_send()
        took(c1.at[r, pl.ds(0, plane - 1)], send_1.at[r])
        took(c2.at[r, pl.ds(0, n_z - 1)], send_2.at[r])
        took(fin.at[pl.ds(0, plane - 1)], send_3.at[r])
        took(fin.at[pl.ds(0, plane)], send_4.at[r])
    took(fin_ref, keep.at[0])
    mark(None)


def finish(geo, sens_ref, fin_ref, out_ref, gin_ref, gout_ref, gb_ref, held, fin, gin, gout, gb, come, go):
    scale, latent, chans = geo
    n = held.shape[0]
    rows = held.shape[2]
    mem = held.shape[1]

    def come_in(i, m):
        return pltpu.make_async_copy(sens_ref.at[m, pl.ds(i * rows, rows), :], held.at[i, m], come.at[mem * i + m])

    def go_out(i, m):
        return pltpu.make_async_copy(held.at[i, m], out_ref.at[m, pl.ds(i * rows, rows), :], go.at[mem * i + m])

    fin_in = pltpu.make_async_copy(fin_ref, fin, come.at[mem * n])
    gin_out = pltpu.make_async_copy(gin, gin_ref, go.at[mem * n])
    gout_out = pltpu.make_async_copy(gout, gout_ref, go.at[mem * n + 1])
    gb_out = pltpu.make_async_copy(gb, gb_ref, go.at[mem * n + 2])
    fin_in.start()
    both = [(i, m) for i in range(n) for m in range(mem)]
    for i, m in both:
        come_in(i, m).start()
    fin_in.wait()
    share = fin.shape[1]
    for r in range(fin.shape[0]):
        gin[r * share:(r + 1) * share, :] = fin[r, :, :latent].astype(F32) * scale
    gin_out.start()
    flipped = fin[:, :, latent:].astype(F32).reshape(gin.shape[0], -1).T * scale
    gout[...] = flipped[:chans, :]
    gb[...] = flipped[chans:chans + 1, :]
    gout_out.start()
    gb_out.start()
    for i, m in both:
        come_in(i, m).wait()
        go_out(i, m).start()
    for i, m in both:
        go_out(i, m).wait()
    gin_out.wait()
    gout_out.wait()
    gb_out.wait()


def on_device(hidden_codes, w_in, b_in, w_out, b_out, target, band_start):
    mem, latent, cells = hidden_codes.shape
    hid = w_in.shape[0]
    chans = w_out.shape[0]
    rows = cells // LON
    n_mem = lax.axis_size("member")
    n_space = lax.axis_size("space")
    n_z = n_space // 4
    plane = 2 * n_mem
    angle = ((band_start[0] + jnp.arange(rows, dtype=jnp.int32)).astype(F32) + 0.5) * (
        math.pi / (rows * n_space)) - math.pi / 2
    area = jnp.cos(angle)
    wide = latent + 128
    half = hid // 2
    block = half // PARTS
    share = block // plane
    vm = pl.BlockSpec(memory_space=pltpu.VMEM)
    hbm = pl.BlockSpec(memory_space=pl.ANY)
    dma = pltpu.SemaphoreType.DMA

    def by_sub(make):
        return [make(2 * size) for size in SUBS]

    sens, fin = pl.pallas_call(
        functools.partial(kernel, (n_mem, n_z, cells)),
        out_shape=(
            jax.ShapeDtypeStruct((mem, cells, latent), BF16),
            jax.ShapeDtypeStruct((2 * PARTS * plane, share, wide), BF16),
        ),
        in_specs=[pl.BlockSpec(memory_space=pltpu.SMEM)] + [hbm] * 6,
        out_specs=(hbm, hbm),
        scratch_shapes=[
            pltpu.VMEM((hid, latent), BF16),
            pltpu.VMEM((1, hid), F32),
            pltpu.VMEM((chans, hid), BF16),
            pltpu.VMEM((1, chans), F32),
            pltpu.VMEM((chans, cells), BF16),
            *by_sub(lambda n: pltpu.VMEM((n_mem, n, latent), BF16)),
            *by_sub(lambda n: pltpu.VMEM((n_mem, hid, n), F32)),
            *by_sub(lambda n: pltpu.VMEM((n_mem, hid, n), BF16)),
            *by_sub(lambda n: pltpu.VMEM((n_mem, chans, n), BF16)),
            *by_sub(lambda n: pltpu.VMEM((n_mem, chans, n), BF16)),
            *by_sub(lambda n: pltpu.VMEM((n_mem, chans, n), BF16)),
            pltpu.VMEM((hid, latent), BF16),
            pltpu.VMEM((latent, hid), BF16),
            pltpu.VMEM((hid, chans), BF16),
            pltpu.VMEM((hid, 128), F32),
            pltpu.VMEM((chans, 128), F32),
            pltpu.VMEM((n_mem, chans, CHUNK), F32),
            pltpu.VMEM((2 * n_mem, chans, CHUNK), F32),
            pltpu.VMEM((hid, latent), F32),
            pltpu.VMEM((hid, 128), F32),
            pltpu.VMEM((hid, 128), F32),
            pltpu.VMEM((PARTS, block, wide), BF16),
            pltpu.VMEM((PARTS, block, wide), BF16),
            pltpu.VMEM((block, wide), F32),
            pltpu.VMEM((PARTS, plane, share, wide), BF16),
            pltpu.VMEM((PARTS, plane, share, wide), BF16),
            pltpu.VMEM((PARTS, share, wide), BF16),
            pltpu.VMEM((PARTS, n_z, share, wide), BF16),
            pltpu.VMEM((2 * PARTS * plane, share, wide), BF16),
            dma((2,)), dma((2,)), dma((2,)), dma((2 * n_mem,)),
            *[dma((PARTS,))] * 10,
            dma((2 * n_mem,)), dma((1,)), dma((1,)), dma((5,)),
        ],
        compiler_params=pltpu.CompilerParams(
            collective_id=0, has_side_effects=True, vmem_limit_bytes=67043328),
    )(area, jnp.swapaxes(hidden_codes, 1, 2), w_in, b_in.reshape(1, hid), w_out, b_out.reshape(1, chans), target)
    pieces = 6
    sens, gin, gout, gb = pl.pallas_call(
        functools.partial(finish, (1.0 / math.sqrt(2 * n_mem * cells), latent, chans)),
        out_shape=(
            jax.ShapeDtypeStruct((mem, cells, latent), BF16),
            jax.ShapeDtypeStruct((hid, latent), F32),
            jax.ShapeDtypeStruct((chans, hid), F32),
            jax.ShapeDtypeStruct((1, hid), F32),
        ),
        in_specs=[hbm, hbm],
        out_specs=(hbm, hbm, hbm, hbm),
        scratch_shapes=[
            pltpu.VMEM((pieces, mem, cells // pieces, latent), BF16),
            pltpu.VMEM((2 * PARTS * plane, share, wide), BF16),
            pltpu.VMEM((hid, latent), F32),
            pltpu.VMEM((chans, hid), F32),
            pltpu.VMEM((1, hid), F32),
            dma((pieces * mem + 1,)), dma((pieces * mem + 3,)),
        ],
    )(sens, fin)
    return jnp.swapaxes(sens, 1, 2), gin, gout, gb.reshape(hid)


def solution(mesh):
    in_specs = (P("member", None, "space"), P(), P(), P(), P(), P(None, "space"), P("space"))
    out_specs = (P("member", None, "space"), P(), P(), P())
    return jax.shard_map(
        on_device, mesh=mesh, in_specs=in_specs, out_specs=out_specs, check_vma=False
    )
```

time: 274 us -> 80.2 us (0.29)
  Pallas kernels: 0 us -> 78.3 us
  waiting for transfers between devices: 66.9 us -> 0 us
  matrix products: 64.1 us -> 0 us
  other arithmetic: 57.3 us -> 0.56 us
  blocking collectives: 46.4 us -> 0 us
  starting transfers between devices: 20.6 us -> 0 us
  local copies, waits for them, and re-layouts: 16.1 us -> 0 us
    pallas_call x0 -> x2, Pallas kernels: none -> 78.3 us  [the longest x1 74.7 us: on_device(): pl.pallas_call(functools.partial(kernel, (n_mem, n_z, cells)), out_shape=...]
    all_to_all x4 -> x0, waiting for transfers between devices: 66.9 us -> none  [the longest x1 28.6 us: copy_for_each(): lax.all_to_all(jnp.broadcast_to(array[None], (devices, *array.shape)), ax...]
    dot_general x12 -> x0, matrix products: 64.1 us -> none  [the longest x2 22.3 us: on_device(): jnp.dot(w_out.T, prediction_adjoint, preferred_element_type=jnp.float32)]
    add x16 -> x0, other arithmetic: 48.1 us -> none  [lone_realization(): return (total + slope(values - other.astype(jnp.float32)[None]), None)]
    all_to_all x2 -> x0, blocking collectives: 46.4 us -> none  [the longest x1 36.3 us: sent_and_summed(): lax.all_to_all(split_up(array, dim, devices), axis, 0, 0, tiled=True)]
    all_to_all x4 -> x0, starting transfers between devices: 20.6 us -> none  [the longest x2 7.48 us: exchange_in_pieces(): lax.all_to_all(piece, axis, split_axis=0, concat_axis=0, tiled=True)]
    convert_element_type x3 -> x0, other arithmetic: 4.54 us -> none  [the longest x1 2.3 us: on_device(): prediction_sensitivity = (area[None, None, :] * (slope(diagonal_contribut...]
    split x2 -> x0, local copies, waits for them, and re-layouts: 4.28 us -> none  [exchange_in_pieces(): jnp.split(parts, edges_of(parts.shape[cut], pieces), axis=cut)]
  transfers between devices with their start and end apart: 4 -> 0, of which waited for: 4 -> 0; matrix products, arithmetic and copies ran while one was open for 6% -> 0% of each run, Pallas kernels for 0% -> 0%
where the time goes in v2:
time: 80.2 us; the launch traced here: 80.1 us
  Pallas kernels  78.3 us (98%)
  between operations  1.29 us (2%)
    pallas_call x1, Pallas kernels, on_device(): pl.pallas_call(functools.partial(kernel, (n_mem, n_z, cells)), out_shape=...  74.7 us
    pallas_call x1, Pallas kernels, on_device(): pl.pallas_call(functools.partial(finish, (1.0 / math.sqrt(2 * n_mem * cel...  3.57 us

profile of v2, /device:TPU:1, one launch (start us, length us, event | category | flops | bytes accessed | tf_op | source)
XLA Modules:
  0.0 80.1 jit_solution(15938550463724754093)
XLA Ops:
  1.3 0.6 add_cosine_fusion.area_ref
  1.8 74.7 %shard_map.102 = (bf16[2,2880,256]{2,1,0:T(8,128)(2,1)}, bf16[64,16,384]{2,1,0:T(8,128)(2,1)}) custom-call(f32[2]{0:T(128)} %add_cosine_fusion.area_ref, bf16[2,2880,256]{2,1,0:T(8,128)(2,1)} %bitcast.7, bf16[1024,256]{1,0:T(8,128)(2,1)} %w_in_hbm.1, f32[1,1024]{1,0:T(1,128)} %bitcast.8, bf16[72,1024]{1,0:T(8,128)(2,1)} %w_out_hbm.1, f32[1,72]{1,0:T(1,128)} %bitcast.9, ...), custom_call_target="tpu_custom_call" | custom-call | tf_op jit(solution)/shard_map/pallas_call | solution.py:498
  76.5 3.6 %shard_map.103 = (bf16[2,2880,256]{2,1,0:T(8,128)(2,1)}, f32[1024,256]{1,0:T(8,128)}, f32[72,1024]{1,0:T(8,128)}, f32[1,1024]{1,0:T(1,128)}) custom-call(bf16[2,2880,256]{2,1,0:T(8,128)(2,1)} %get-tuple-element.10.sens_ref, bf16[64,16,384]{2,1,0:T(8,128)(2,1)} %get-tuple-element.11.fin_ref), custom_call_target="tpu_custom_call" | custom-call | tf_op jit(solution)/shard_map/pallas_call | solution.py:544

commit v3 on v2

--- a/solution.py
+++ b/solution.py
@@ -11,8 +11,10 @@
 LON = 1440
 SUBS = (256, 128)
 CHUNK = sum(SUBS)
-PARTS = 2
-LATE = 2
+PARTS = 4
+LATE = 3
+CUT_F = 8
+CUT_B = 1
 MESH = pl.DeviceIdType.MESH
 K0 = math.sqrt(2.0 / math.pi)
 K1 = K0 * 0.044715
@@ -35,18 +37,17 @@
 
 def kernel(
     geo,
-    area_ref, h_ref, w_in_hbm, b_in_hbm, w_out_hbm, b_out_hbm, target_hbm,
+    band_ref, h_ref, w_in_ref, b_in_ref, w_out_ref, b_out_ref, target_ref,
     sens_ref, fin_ref,
-    w_in_ref, b_in_ref, w_out_ref, b_out_ref, target_ref,
     hs0, hs1, slopes0, slopes1, acts0, acts1, fcast0, fcast1, fpart0, fpart1, dback0, dback1,
-    w_half, w_in_t, w_out_t, bias, bias_out, goal, ftile,
+    areas, w_half, w_in_t, w_out_t, bias, bias_out, goal, ftile,
     acc_in, acc_out, acc_b, gsend, c0, own, p1, c1, z1, c2, fin,
     send_a, recv_a, send_b, recv_b, send_0, recv_0, send_1, recv_1, send_2, recv_2, send_3, recv_3, send_4, recv_4,
-    load, store, keep, given,
+    load, store, keep,
 ):
-    n_mem, n_z, cells = geo
-    hid, latent = w_in_hbm.shape
-    chans = w_out_hbm.shape[0]
+    n_mem, n_z, cells, lat_rows = geo
+    hid, latent = w_in_ref.shape
+    chans = w_out_ref.shape[0]
     hs, slopes, acts = (hs0, hs1), (slopes0, slopes1), (acts0, acts1)
     fcast, fpart, dback = (fcast0, fcast1), (fpart0, fpart1), (dback0, dback1)
     me = lax.axis_index("member")
@@ -72,13 +73,6 @@
     mark = Mark()
     mark('entry')
 
-    weights = [
-        pltpu.make_async_copy(far, near, given.at[i]) for i, (far, near) in enumerate((
-            (w_in_hbm, w_in_ref), (w_out_hbm, w_out_ref), (b_in_hbm, b_in_ref), (b_out_hbm, b_out_ref),
-            (target_hbm, target_ref)))]
-    for copy in weights:
-        copy.start()
-
     def pieces(c, b, size):
         return [(m, pl.ds(c * CHUNK + first_at[b], size), pl.ds(m * SUBS[b], size)) for m in range(2)]
 
@@ -109,8 +103,6 @@
     pl.semaphore_signal(barrier, inc=1, device_id=partner, device_id_type=MESH)
 
     mark('prep')
-    for copy in weights:
-        copy.wait()
     for m in range(2):
         hs0[full, m * SUBS[0] + rest:(m + 1) * SUBS[0], :] = jnp.zeros((SUBS[0] - rest, latent), BF16)
     for c in range(n_mem):
@@ -120,6 +112,10 @@
             goal[c] = jnp.concatenate(
                 [target_ref[:, c * CHUNK:cells].astype(F32), jnp.zeros((chans, CHUNK - rest), F32)], axis=1)
     w_in_t[...] = w_in_ref[...].T
+    cell = me * CHUNK + lax.broadcasted_iota(jnp.int32, (8, CHUNK), 1)
+    row = band_ref[0] + jnp.where(cell < LON, 0, 1)
+    angle = (row.astype(F32) + 0.5) * (math.pi / lat_rows) - math.pi / 2
+    areas[...] = jnp.where(cell < cells, jnp.cos(angle), 0.0)
     w_half[...] = w_in_ref[...] * 0.5
     w_out_t[...] = w_out_ref[...].T * 0.5
     bias[...] = jnp.broadcast_to(0.5 * b_in_ref[...], (128, hid)).T
@@ -201,16 +197,14 @@
 
         return carry
 
-    lax.fori_loop(0, n_mem, forward1, 0)
-
-    lanes = lax.broadcasted_iota(jnp.int32, (8, 128), 1)
 
     def meet(b):
         size = SUBS[b]
         at = first_at[b]
         fpart[b][me] = fcast[b][me]
         took(fpart[b].at[pl.ds(0, n_mem - 1)], recv_a.at[b])
-        mark(f'pairs{b}')
+        if b == 0:
+            mark('pairs0')
         for p in range(n_mem):
             for m in range(2):
                 ftile[2 * p + m, :, at:at + size] = fpart[b][p, :, m * size:(m + 1) * size].astype(F32)
@@ -219,8 +213,7 @@
             rows = pl.ds(pl.multiple_of(r * 8, 8), 8)
             for k in range(size // 128):
                 cols = slice(at + k * 128, at + (k + 1) * 128)
-                cell = me * CHUNK + (at + k * 128) + lanes
-                area = jnp.where(cell < LON, area_ref[0], jnp.where(cell < 2 * LON, area_ref[1], 0.0))
+                area = areas[:, cols]
                 f = [ftile[i, rows, cols] for i in range(2 * n_mem)]
                 total = [None] * (2 * n_mem)
                 for i in range(2 * n_mem):
@@ -245,54 +238,62 @@
             b_copy(b, d, me).start()
         dback[b][me] = fpart[b][me]
 
+    def backward_chunk(b, *chunks):
+        acc_out[:, :chans] += sum(
+            lax.dot_general(acts[b][c], dback[b][c], (((1,), (1,)), ((), ())), preferred_element_type=F32)
+            for c in chunks)
+        for c in chunks:
+            for j in range(2 * SUBS[b] // 256):
+                cols = slice(j * 256, (j + 1) * 256)
+                dact = jnp.dot(w_out_t[...], dback[b][c, :, cols], preferred_element_type=F32)
+                dpre = (dact * slopes[b][c, :, cols]).astype(BF16)
+                acts[b][c, :, cols] = dpre
+                wide = dpre.astype(F32)
+                acc_b[...] += wide[:, :128] + wide[:, 128:]
+        acc_in[...] += sum(jnp.dot(acts[b][c], hs[b][c], preferred_element_type=F32) for c in chunks)
+
+    def backward0(step, carry):
+        c = lax.rem(me + n_mem - step, n_mem)
+
+        @pl.when(step > 0)
+        def _():
+            b_copy(0, c, c).wait_recv()
+
+        backward_chunk(0, c)
+        return carry
+
+    def second(i):
+        c = lax.rem(jnp.minimum(me, full - 1) + full - i, full)
+
+        @pl.when(c != me)
+        def _():
+            b_copy(1, c, c).wait_recv()
+
+        return c
+
+    def backward1(step, carry):
+        backward_chunk(1, second(2 * step), second(2 * step + 1))
+        return carry
+
+    lax.fori_loop(0, CUT_F, forward1, 0)
     mark('waitA0')
     meet(0)
+    mark('forward1b')
+    lax.fori_loop(CUT_F, n_mem, forward1, 0)
+    mark('backward0')
+    lax.fori_loop(0, CUT_B, backward0, 0)
     mark('waitA1')
 
     @pl.when(me < full)
     def _():
         meet(1)
 
-    def backward_chunk(b, c):
-        d = dback[b][c]
-        acc_out[:, :chans] += lax.dot_general(
-            acts[b][c], d, (((1,), (1,)), ((), ())), preferred_element_type=F32)
-        for j in range(2 * SUBS[b] // 256):
-            cols = slice(j * 256, (j + 1) * 256)
-            dact = jnp.dot(w_out_t[...], d[:, cols], preferred_element_type=F32)
-            dpre = (dact * slopes[b][c, :, cols]).astype(BF16)
-            acts[b][c, :, cols] = dpre
-            wide = dpre.astype(F32)
-            acc_b[...] += wide[:, :128] + wide[:, 128:]
-        acc_in[...] += jnp.dot(acts[b][c], hs[b][c], preferred_element_type=F32)
-
-    def backward0(step, carry):
-        c = lax.rem(me + n_mem - step, n_mem)
-
-        @pl.when(step > 0)
-        def _():
-            b_copy(0, c, c).wait_recv()
-
-        backward_chunk(0, c)
-        return carry
-
-    def backward1(step, carry):
-        c = lax.rem(me + n_mem - step, n_mem)
-
-        @pl.when(c < full)
-        def _():
-            @pl.when(step > 0)
-            def _():
-                b_copy(1, c, c).wait_recv()
-
-            backward_chunk(1, c)
-
-        return carry
-
-    mark('backward0')
-    lax.fori_loop(0, n_mem, backward0, 0)
+    mark('backward0b')
+    lax.fori_loop(CUT_B, n_mem, backward0, 0)
     mark('backward1')
-    lax.fori_loop(0, n_mem, backward1, 0)
+    lax.fori_loop(0, full // 2, backward1, 0)
+    for i in range(full // 2 * 2, full):
+        backward_chunk(1, second(i))
 
     def sens_of(*chunks):
         for c in chunks:
@@ -481,9 +482,6 @@
     n_space = lax.axis_size("space")
     n_z = n_space // 4
     plane = 2 * n_mem
-    angle = ((band_start[0] + jnp.arange(rows, dtype=jnp.int32)).astype(F32) + 0.5) * (
-        math.pi / (rows * n_space)) - math.pi / 2
-    area = jnp.cos(angle)
     wide = latent + 128
     half = hid // 2
     block = half // PARTS
@@ -496,25 +494,21 @@
         return [make(2 * size) for size in SUBS]
 
     sens, fin = pl.pallas_call(
-        functools.partial(kernel, (n_mem, n_z, cells)),
+        functools.partial(kernel, (n_mem, n_z, cells, rows * n_space)),
         out_shape=(
             jax.ShapeDtypeStruct((mem, cells, latent), BF16),
             jax.ShapeDtypeStruct((2 * PARTS * plane, share, wide), BF16),
         ),
-        in_specs=[pl.BlockSpec(memory_space=pltpu.SMEM)] + [hbm] * 6,
+        in_specs=[pl.BlockSpec(memory_space=pltpu.SMEM), hbm] + [vm] * 5,
         out_specs=(hbm, hbm),
         scratch_shapes=[
-            pltpu.VMEM((hid, latent), BF16),
-            pltpu.VMEM((1, hid), F32),
-            pltpu.VMEM((chans, hid), BF16),
-            pltpu.VMEM((1, chans), F32),
-            pltpu.VMEM((chans, cells), BF16),
             *by_sub(lambda n: pltpu.VMEM((n_mem, n, latent), BF16)),
             *by_sub(lambda n: pltpu.VMEM((n_mem, hid, n), F32)),
             *by_sub(lambda n: pltpu.VMEM((n_mem, hid, n), BF16)),
             *by_sub(lambda n: pltpu.VMEM((n_mem, chans, n), BF16)),
             *by_sub(lambda n: pltpu.VMEM((n_mem, chans, n), BF16)),
             *by_sub(lambda n: pltpu.VMEM((n_mem, chans, n), BF16)),
+            pltpu.VMEM((8, CHUNK), F32),
             pltpu.VMEM((hid, latent), BF16),
             pltpu.VMEM((latent, hid), BF16),
             pltpu.VMEM((hid, chans), BF16),
@@ -535,11 +529,11 @@
             pltpu.VMEM((2 * PARTS * plane, share, wide), BF16),
             dma((2,)), dma((2,)), dma((2,)), dma((2 * n_mem,)),
             *[dma((PARTS,))] * 10,
-            dma((2 * n_mem,)), dma((1,)), dma((1,)), dma((5,)),
+            dma((2 * n_mem,)), dma((1,)), dma((1,)),
         ],
         compiler_params=pltpu.CompilerParams(
             collective_id=0, has_side_effects=True, vmem_limit_bytes=67043328),
-    )(area, jnp.swapaxes(hidden_codes, 1, 2), w_in, b_in.reshape(1, hid), w_out, b_out.reshape(1, chans), target)
+    )(band_start, jnp.swapaxes(hidden_codes, 1, 2), w_in, b_in.reshape(1, hid), w_out, b_out.reshape(1, chans), target)
     pieces = 6
     sens, gin, gout, gb = pl.pallas_call(
         functools.partial(finish, (1.0 / math.sqrt(2 * n_mem * cells), latent, chans)),

time: 80.2 us -> 77.1 us (0.961)
  Pallas kernels: 78.3 us -> 75.5 us
    pallas_call x1, Pallas kernels: 74.7 us -> 71.9 us  [on_device(): pl.pallas_call(functools.partial(kernel, (n_mem, n_z, cells, rows * n_spa...]
where the time goes in v3:
time: 77.1 us; the launch traced here: 77 us
  Pallas kernels  75.5 us (98%)
  between operations  1.45 us (2%)
    pallas_call x1, Pallas kernels, on_device(): pl.pallas_call(functools.partial(kernel, (n_mem, n_z, cells, rows * n_spa...  71.9 us
    pallas_call x1, Pallas kernels, on_device(): pl.pallas_call(functools.partial(finish, (1.0 / math.sqrt(2 * n_mem * cel...  3.57 us

profile of v3, /device:TPU:1, one launch (start us, length us, event | category | flops | bytes accessed | tf_op | source)
XLA Modules:
  0.0 77.0 jit_solution(5740076600789371962)
XLA Ops:
  1.3 71.9 %shard_map.102 = (bf16[2,2880,256]{2,1,0:T(8,128)(2,1)}, bf16[128,8,384]{2,1,0:T(8,128)(2,1)}) custom-call(s32[1]{0:T(128)S(6)} %copy.11.band_ref, bf16[2,2880,256]{2,1,0:T(8,128)(2,1)} %bitcast.5, bf16[1024,256]{1,0:T(8,128)(2,1)} %w_in_ref.1, f32[1,1024]{1,0:T(1,128)} %bitcast.6, bf16[72,1024]{1,0:T(8,128)(2,1)} %w_out_ref.1, f32[1,72]{1,0:T(1,128)} %bitcast.7, ...), custom_call_target="tpu_custom_call" | custom-call | tf_op jit(solution)/shard_map/pallas_call | solution.py:496
  73.2 3.6 %shard_map.103 = (bf16[2,2880,256]{2,1,0:T(8,128)(2,1)}, f32[1024,256]{1,0:T(8,128)}, f32[72,1024]{1,0:T(8,128)}, f32[1,1024]{1,0:T(1,128)}) custom-call(bf16[2,2880,256]{2,1,0:T(8,128)(2,1)} %get-tuple-element.10.sens_ref, bf16[128,8,384]{2,1,0:T(8,128)(2,1)} %get-tuple-element.11.fin_ref), custom_call_target="tpu_custom_call" | custom-call | tf_op jit(solution)/shard_map/pallas_call | solution.py:538

commit v4 on v3

--- a/solution.py
+++ b/solution.py
@@ -129,6 +129,11 @@
             src_ref=fcast[b].at[d], dst_ref=fpart[b].at[slot], send_sem=send_a.at[b],
             recv_sem=recv_a.at[b], device_id={"member": d}, device_id_type=MESH)
 
+    def b_piece(b, d, piece):
+        return pltpu.make_async_remote_copy(
+            src_ref=fpart[b].at[d, piece, :], dst_ref=dback[b].at[me, piece, :], send_sem=send_b.at[b],
+            recv_sem=recv_b.at[b * n_mem + me], device_id={"member": d}, device_id_type=MESH)
+
     def b_copy(b, d, slot):
         return pltpu.make_async_remote_copy(
             src_ref=fpart[b].at[d], dst_ref=dback[b].at[slot], send_sem=send_b.at[b],
@@ -229,13 +234,16 @@
                     ftile[i, rows, cols] = area * (v - total[i] * (1.0 / (2 * n_mem)))
             return carry
 
-        lax.fori_loop(0, chans // 8, pairs, 0)
-        for p in range(n_mem):
-            for m in range(2):
-                fpart[b][p, :, m * size:(m + 1) * size] = ftile[2 * p + m, :, at:at + size].astype(BF16)
-        for off in range(1, n_mem):
-            d = lax.rem(me + off, n_mem)
-            b_copy(b, d, me).start()
+        lo = 0
+        for hi in (chans // 16 * 8, chans):
+            lax.fori_loop(lo // 8, hi // 8, pairs, 0)
+            piece = slice(lo, hi)
+            for p in range(n_mem):
+                for m in range(2):
+                    fpart[b][p, piece, m * size:(m + 1) * size] = ftile[2 * p + m, piece, at:at + size].astype(BF16)
+            for off in range(1, n_mem):
+                b_piece(b, lax.rem(me + off, n_mem), pl.ds(lo, hi - lo)).start()
+            lo = hi
         dback[b][me] = fpart[b][me]
 
     def backward_chunk(b, *chunks):
@@ -272,7 +280,7 @@
         return c
 
     def backward1(step, carry):
-        backward_chunk(1, second(2 * step), second(2 * step + 1))
+        backward_chunk(1, second(2 * step + 1), second(2 * step + 2))
         return carry
 
     lax.fori_loop(0, CUT_F, forward1, 0)
@@ -288,12 +296,18 @@
     def _():
         meet(1)
 
+    @pl.when(me < full)
+    def _():
+        backward_chunk(1, me)
+
     mark('backward0b')
     lax.fori_loop(CUT_B, n_mem, backward0, 0)
     mark('backward1')
-    lax.fori_loop(0, full // 2, backward1, 0)
-    for i in range(full // 2 * 2, full):
-        backward_chunk(1, second(i))
+    lax.fori_loop(0, (full - 1) // 2, backward1, 0)
+
+    @pl.when(me == full)
+    def _():
+        backward_chunk(1, second(0))
 
     def sens_of(*chunks):
         for c in chunks:

time: 77.1 us -> 75.2 us (0.975)
  Pallas kernels: 75.5 us -> 73.6 us
    pallas_call x1, Pallas kernels: 71.9 us -> 70 us  [on_device(): pl.pallas_call(functools.partial(kernel, (n_mem, n_z, cells, rows * n_spa...]
where the time goes in v4:
time: 75.2 us; the launch traced here: 75 us
  Pallas kernels  73.6 us (98%)
  between operations  1.45 us (2%)
    pallas_call x1, Pallas kernels, on_device(): pl.pallas_call(functools.partial(kernel, (n_mem, n_z, cells, rows * n_spa...  70 us
    pallas_call x1, Pallas kernels, on_device(): pl.pallas_call(functools.partial(finish, (1.0 / math.sqrt(2 * n_mem * cel...  3.57 us

profile of v4, /device:TPU:1, one launch (start us, length us, event | category | flops | bytes accessed | tf_op | source)
XLA Modules:
  0.0 75.0 jit_solution(7789871850621828247)
XLA Ops:
  1.3 70.0 %shard_map.102 = (bf16[2,2880,256]{2,1,0:T(8,128)(2,1)}, bf16[128,8,384]{2,1,0:T(8,128)(2,1)}) custom-call(s32[1]{0:T(128)S(6)} %copy.11.band_ref, bf16[2,2880,256]{2,1,0:T(8,128)(2,1)} %bitcast.5, bf16[1024,256]{1,0:T(8,128)(2,1)} %w_in_ref.1, f32[1,1024]{1,0:T(1,128)} %bitcast.6, bf16[72,1024]{1,0:T(8,128)(2,1)} %w_out_ref.1, f32[1,72]{1,0:T(1,128)} %bitcast.7, ...), custom_call_target="tpu_custom_call" | custom-call | tf_op jit(solution)/shard_map/pallas_call | solution.py:510
  71.3 3.6 %shard_map.103 = (bf16[2,2880,256]{2,1,0:T(8,128)(2,1)}, f32[1024,256]{1,0:T(8,128)}, f32[72,1024]{1,0:T(8,128)}, f32[1,1024]{1,0:T(1,128)}) custom-call(bf16[2,2880,256]{2,1,0:T(8,128)(2,1)} %get-tuple-element.10.sens_ref, bf16[128,8,384]{2,1,0:T(8,128)(2,1)} %get-tuple-element.11.fin_ref), custom_call_target="tpu_custom_call" | custom-call | tf_op jit(solution)/shard_map/pallas_call | solution.py:552
